TPU v7x, 1024 devices: a whole 8x8x8 slice. The times are simulated.
1024 devices in a mesh: row: 16 (over x, core), grp: 64 (over y, z).
Axes of the slice: x: 8, y: 8, z: 8, core: 2. Of those that a mesh axis runs over, the one named last changes fastest.
Arguments:
- integrals: bfloat16 [1024, 512, 256], P('grp', 'row'), may hold values from -1.1953125 to 1.1953125
- amplitudes: bfloat16 [256, 4096, 256], P('grp', 'row'), may hold values from -1.796875 to 1.796875
- pair_orbs: int32 [256, 32], P('grp', 'row'), may hold values from 0 to 15, as said below
- pair_count: int32 [64, 16], P('grp', 'row'), may hold values from 1 to 4, as said below
- neighbours: int32 [256, 64], P('grp', 'row'), may hold values from 0 to 11
- coupling: float32 [256, 64], P('grp', 'row'), may hold values from -1.8 to 1.8
- bases: bfloat16 [256, 4096, 256], P('grp', 'row'), may hold values from -0.375 to 0.375
- virt_energy: float32 [256, 4096], P('grp', 'row'), may hold values from 0.3 to 3
- occ_energy: float32 [256, 16], P('grp', 'row'), may hold values from -1.5 to -0.3
Outputs:
- residual: float32 [256, 4096, 256], P('grp', 'row')
Inputs may be any that keep to these rules, and one draw needn't show every extreme that they name: `pair_orbs`: in the columns of row r the first orbital of every pair is orbital r of the group, the one owned by that device; the second is any orbital of the group. `pair_count`: live slots come first on each device; some device holds 4 live pairs in every draw.
All inputs are finite; a program needn't handle non-finite values.
Results may differ from a plain program's by a relative error of at most 0.0007.
Values may be sent and summed in bfloat16 or wider, within the bound.
A program may use at most 32 MiB of HBM per device.

v0:
```python
import jax
import jax.numpy as jnp
from jax import lax
from jax.sharding import PartitionSpec as P


def with_halo(array, sides, width):
    for axis, dim in sides:
        count, length = (lax.axis_size(axis), array.shape[dim])
        up = [(i, (i + 1) % count) for i in range(count - 1)]
        down = [(j, i) for i, j in up]
        last = lax.slice_in_dim(array, length - width, length, axis=dim)
        initial = lax.slice_in_dim(array, 0, width, axis=dim)
        before = lax.ppermute(last, axis, up)
        after = lax.ppermute(initial, axis, down)
        array = jnp.concatenate([before, array, after], axis=dim)
    return array


def local(
    integrals,
    amplitudes,
    pair_orbs,
    pair_count,
    neighbours,
    coupling,
    bases,
    virt_energy,
    occ_energy,
):
    width = amplitudes.shape[0]
    live = jnp.arange(width, dtype=jnp.int32) < pair_count[0, 0]
    amps = jnp.where(live[:, None, None], amplitudes, jnp.zeros((), jnp.bfloat16))
    first_orb = pair_orbs[:, 0]
    second_orb = pair_orbs[:, 1]
    piece = lax.all_gather(integrals, "row", axis=1, tiled=True)
    left = jnp.take(piece, first_orb, axis=0)
    right = jnp.take(piece, second_orb, axis=0)
    integ = jnp.einsum("pxa,pxb->pab", left, right, preferred_element_type=jnp.float32)
    first = jnp.einsum("pac,pcd->pad", bases, amps, preferred_element_type=jnp.float32).astype(
        jnp.bfloat16
    )
    moved = jnp.einsum("pad,pbd->pab", first, bases, preferred_element_type=jnp.float32).astype(
        jnp.bfloat16
    )
    window = with_halo(moved, (("grp", 0),), width)
    onehot = (neighbours[:, :, None] == jnp.arange(3 * width, dtype=jnp.int32)).astype(jnp.float32)
    weights = jnp.sum(coupling[:, :, None] * onehot, axis=1)
    combined = jnp.einsum(
        "pm,mab->pab", weights, window.astype(jnp.float32), precision=lax.Precision.HIGHEST
    ).astype(jnp.bfloat16)
    back_first = jnp.einsum(
        "pca,pcb->pab", bases, combined, preferred_element_type=jnp.float32
    ).astype(jnp.bfloat16)
    back = jnp.einsum("pac,pcb->pab", back_first, bases, preferred_element_type=jnp.float32)
    denom = virt_energy[:, :, None] + virt_energy[:, None, :] - occ_energy[:, :, None]
    resid = integ + denom * amps.astype(jnp.float32) - back
    return jnp.where(live[:, None, None], resid, jnp.zeros((), jnp.float32))


def solution(mesh):
    placed = (
        P("grp", "row", None),
        P("grp", "row", None),
        P("grp", "row"),
        P("grp", "row"),
        P("grp", "row"),
        P("grp", "row"),
        P("grp", "row", None),
        P("grp", "row"),
        P("grp", "row"),
    )
    return jax.shard_map(
        local, mesh=mesh, in_specs=placed, out_specs=P("grp", "row", None), check_vma=False
    )
```

profile of v0, /device:TPU:1, one launch (start us, length us, event | category | flops | bytes accessed | tf_op | source)
XLA Modules:
  0.0 87.4 jit_solution(15903632552987506571)
XLA Ops:
  6.5 0.0 copy-start
  6.5 0.0 copy-start.3
  6.5 0.0 copy-start.2
  6.5 0.0 copy-start.1
  6.5 0.0 all-gather.2.cloned.1.call-start
  6.6 0.7 all-gather.2.cloned.1.call-update
  7.9 0.0 copy-done
  7.9 1.5 %convolution_convert_fusion.2 = bf16[4,256,256]{2,1,0:T(8,128)(2,1)S(1)} fusion(bf16[4,256,256]{2,1,0:T(8,128)(2,1)S(1)} %copy-done, bf16[4,256,256]{2,1,0:T(8,128)(2,1)} %param.12, pred[4]{0:T(512)(128)(4,1)S(1)} %iota_compare_fusion.1), kind=kOutput, calls=%fused_computation.10 | convolution fusion | flops 269221888 | bytes 1572868 | tf_op jit(solution)/shard_map/pad,pbd->pab/dot_general | solution.py:43
  9.5 5.8 %collective-permute-start = (bf16[4,256,256]{2,1,0:T(8,128)(2,1)S(1)}, bf16[4,256,256]{2,1,0:T(8,128)(2,1)S(1)}, u32[]{:S(2)}, u32[]{:S(2)}) collective-permute-start(bf16[4,256,256]{2,1,0:T(8,128)(2,1)S(1)} %convolution_convert_fusion.2), channel_id=1, source_target_pairs={{0,1},{1,2},{2,3},{3,4},{4,5},{5,6},{6,7},{7,8},{8,9},{9,10},{10,1... | collective-permute-start | bytes 1572872 | tf_op jit(solution)/shard_map/ppermute | solution.py:14
  15.3 1.3 %collective-permute-start.1 = (bf16[4,256,256]{2,1,0:T(8,128)(2,1)S(1)}, bf16[4,256,256]{2,1,0:T(8,128)(2,1)S(1)}, u32[]{:S(2)}, u32[]{:S(2)}) collective-permute-start(bf16[4,256,256]{2,1,0:T(8,128)(2,1)S(1)} %convolution_convert_fusion.2), channel_id=1, source_target_pairs={{1,0},{2,1},{3,2},{4,3},{5,4},{6,5},{7,6},{8,7},{9,8},{10,9},{11,1... | collective-permute-start | bytes 1572872 | tf_op jit(solution)/shard_map/ppermute | solution.py:15
  16.6 0.0 copy-done.3
  16.6 0.0 copy-done.2
  16.6 0.0 copy-done.1
  16.6 0.1 select_reduce_fusion
  16.7 4.6 %collective-permute-done = bf16[4,256,256]{2,1,0:T(8,128)(2,1)S(1)} collective-permute-done((bf16[4,256,256]{2,1,0:T(8,128)(2,1)S(1)}, bf16[4,256,256]{2,1,0:T(8,128)(2,1)S(1)}, u32[]{:S(2)}, u32[]{:S(2)}) %collective-permute-start) | collective-permute-done | bytes 524320 | tf_op jit(solution)/shard_map/ppermute | solution.py:14
  21.3 5.4 %collective-permute-done.1 = bf16[4,256,256]{2,1,0:T(8,128)(2,1)S(1)} collective-permute-done((bf16[4,256,256]{2,1,0:T(8,128)(2,1)S(1)}, bf16[4,256,256]{2,1,0:T(8,128)(2,1)S(1)}, u32[]{:S(2)}, u32[]{:S(2)}) %collective-permute-start.1) | collective-permute-done | bytes 524320 | tf_op jit(solution)/shard_map/ppermute | solution.py:15
  26.7 0.2 pad_maximum_fusion
  26.9 1.6 %fusion = bf16[4,256,256]{2,0,1:T(4,128)(2,1)S(1)} fusion(bf16[12,256,256]{2,1,0:T(8,128)(2,1)S(1)} %pad_maximum_fusion, f32[4,12]{1,0:T(4,128)S(1)} %select_reduce_fusion), kind=kOutput, calls=%fused_computation.2 | convolution fusion | flops 37748736 | bytes 2097344 | tf_op jit(solution)/shard_map/pm,mab->pab/dot_general | solution.py:49
  28.5 41.1 %all-gather.2.cloned.1.call-done = bf16[16,512,256]{2,1,0:T(8,128)(2,1)} async-done(((bf16[16,32,256]{2,1,0:T(8,128)(2,1)}), bf16[16,512,256]{2,1,0:T(8,128)(2,1)}) %all-gather.2.cloned.1.call-update) | async-done | bytes 4194320 | tf_op jit(solution)/shard_map/all_gather | solution.py:36
  69.5 2.8 %gather_fusion = bf16[4,512,256]{2,1,0:T(8,128)(2,1)S(1)} fusion(bf16[16,512,256]{2,1,0:T(8,128)(2,1)} %all-gather.2.cloned.1.call-done, s32[1024]{0:T(1024)S(1)} %get-tuple-element.13), kind=kCustom, calls=%fused_computation.clone | custom fusion | bytes 2097168 | tf_op jit(solution)/shard_map/jit(_take)/gather | solution.py:37
  72.3 0.0 copy-start.4
  72.3 0.0 copy-start.5
  72.4 2.8 %gather_fusion.1 = bf16[4,512,256]{2,1,0:T(8,128)(2,1)S(1)} fusion(bf16[16,512,256]{2,1,0:T(8,128)(2,1)} %all-gather.2.cloned.1.call-done, s32[1024]{0:T(1024)S(1)} %get-tuple-element.12), kind=kCustom, calls=%fused_computation.1.clone | custom fusion | bytes 2097168 | tf_op jit(solution)/shard_map/jit(_take)/gather | solution.py:38
  75.2 0.0 copy-done.4
  75.2 0.0 copy-done.5
  75.2 2.7 %convolution_add_fusion = f32[4,256,256]{2,1,0:T(8,128)} fusion(bf16[4,512,256]{2,1,0:T(8,128)(2,1)S(1)} %gather_fusion.1, bf16[4,512,256]{2,1,0:T(8,128)(2,1)S(1)} %gather_fusion, pred[4]{0:T(512)(128)(4,1)S(1)} %get-tuple-element.10, pred[4]{0:T(512)(128)(4,1)S(1)} %get-tuple-element.6, f32[4]{0:T(128)S(1)} %bitcast.16, f32[4,256]{1,0:T(4,128)S(1)} %copy-done.4, ...), kind=kOutput, calls=%fused_computation.6 | convolution fusion | flops 271056896 | bytes 3674140 | tf_op jit(solution)/shard_map/pxa,pxb->pab/dot_general | solution.py:39
  77.9 2.7 %fusion.2 = f32[4,256,256]{2,1,0:T(8,128)} fusion(f32[4,256,256]{2,1,0:T(8,128)} %convolution_add_fusion, bf16[4,256,256]{2,1,0:T(8,128)(2,1)S(1)} %copy-done, bf16[4,256,256]{2,0,1:T(4,128)(2,1)S(1)} %fusion, pred[4]{0:T(512)(128)(4,1)S(1)} %iota_compare_fusion.1), kind=kOutput, calls=%fused_computation.7 | convolution fusion | flops 269221888 | bytes 3145732 | tf_op jit(solution)/shard_map/pac,pcb->pab/dot_general | solution.py:55
  (3 shorter events, 0.0 us)
Async XLA Ops:
  6.5 1.4 %copy-start = (bf16[4,256,256]{2,1,0:T(8,128)(2,1)S(1)}, bf16[4,256,256]{2,1,0:T(8,128)(2,1)}, u32[]{:S(2)}) copy-start(bf16[4,256,256]{2,1,0:T(8,128)(2,1)} %param.17) | copy-start | bytes 1572868
  6.5 10.0 %copy-start.3 = (s32[4,2]{0,1:T(2,128)S(1)}, s32[4,2]{0,1:T(2,128)}, u32[]{:S(2)}) copy-start(s32[4,2]{0,1:T(2,128)} %param.13) | copy-start | bytes 100
  6.5 10.1 %copy-start.2 = (s32[4,4]{1,0:T(4,128)S(1)}, s32[4,4]{1,0:T(4,128)}, u32[]{:S(2)}) copy-start(s32[4,4]{1,0:T(4,128)} %param.15) | copy-start | bytes 196
  6.5 10.1 %copy-start.1 = (f32[4,4]{1,0:T(4,128)S(1)}, f32[4,4]{1,0:T(4,128)}, u32[]{:S(2)}) copy-start(f32[4,4]{1,0:T(4,128)} %param.16) | copy-start | bytes 196
  6.5 63.0 %all-gather.2.cloned.1.call-start = ((), (), s32[]{:S(2)}) async-start(), calls=%async_computation | async-start | bytes 4456448 | tf_op jit(solution)/shard_map/all_gather | solution.py:36
  9.5 11.8 %collective-permute-start = (bf16[4,256,256]{2,1,0:T(8,128)(2,1)S(1)}, bf16[4,256,256]{2,1,0:T(8,128)(2,1)S(1)}, u32[]{:S(2)}, u32[]{:S(2)}) collective-permute-start(bf16[4,256,256]{2,1,0:T(8,128)(2,1)S(1)} %convolution_convert_fusion.2), channel_id=1, source_target_pairs={{0,1},{1,2},{2,3},{3,4},{4,5},{5,6},{6,7},{7,8},{8,9},{9,10},{10,1... | collective-permute-start | bytes 1572872 | tf_op jit(solution)/shard_map/ppermute | solution.py:14
  15.3 11.4 %collective-permute-start.1 = (bf16[4,256,256]{2,1,0:T(8,128)(2,1)S(1)}, bf16[4,256,256]{2,1,0:T(8,128)(2,1)S(1)}, u32[]{:S(2)}, u32[]{:S(2)}) collective-permute-start(bf16[4,256,256]{2,1,0:T(8,128)(2,1)S(1)} %convolution_convert_fusion.2), channel_id=1, source_target_pairs={{1,0},{2,1},{3,2},{4,3},{5,4},{6,5},{7,6},{8,7},{9,8},{10,9},{11,1... | collective-permute-start | bytes 1572872 | tf_op jit(solution)/shard_map/ppermute | solution.py:15
  72.3 2.8 %copy-start.4 = (f32[4,256]{1,0:T(4,128)S(1)}, f32[4,256]{1,0:T(4,128)}, u32[]{:S(2)}) copy-start(f32[4,256]{1,0:T(4,128)} %param.18) | copy-start | bytes 12292
  72.3 2.8 %copy-start.5 = (f32[4,1]{0,1:T(1,128)S(1)}, f32[4,1]{0,1:T(1,128)}, u32[]{:S(2)}) copy-start(f32[4,1]{0,1:T(1,128)} %param.19) | copy-start | bytes 52
Sparse Core Ops, SparseCore 0:
  10.1 59.4 all-gather.1
where the time goes:
time: 87.8 us; the launch traced here: 87.4 us
  waiting for transfers between devices  51.7 us (59%)
  between operations  14.2 us (16%)
  matrix products  8.51 us (10%)
  starting transfers between devices  7.09 us (8%)
  local copies, waits for them, and re-layouts  5.64 us (6%)
    all_gather x1, waiting for transfers between devices, local(): piece = lax.all_gather(integrals, 'row', axis=1, tiled=True)  41.1 us
    ppermute x1, starting transfers between devices, with_halo(): before = lax.ppermute(last, axis, up)  5.76 us
    ppermute x1, waiting for transfers between devices, with_halo(): after = lax.ppermute(initial, axis, down)  5.36 us
    ppermute x1, waiting for transfers between devices, with_halo(): before = lax.ppermute(last, axis, up)  4.62 us
    gather x1, local copies, waits for them, and re-layouts, local(): right = jnp.take(piece, second_orb, axis=0)  2.81 us
    gather x1, local copies, waits for them, and re-layouts, local(): left = jnp.take(piece, first_orb, axis=0)  2.8 us
    dot_general x1, matrix products, local(): jnp.einsum('pxa,pxb->pab', left, right, preferred_element_type=jnp.float32)  2.7 us
    dot_general x1, matrix products, local(): jnp.einsum('pac,pcb->pab', back_first, bases, preferred_element_type=jnp....  2.69 us
  transfers between devices with their start and end apart: 3, of which 3 were waited for; matrix products, arithmetic and copies ran while one was open for 4% of the time, Pallas kernels for 0%

commit v1 on v0

v1 whole, which is shorter than its diff:
```python
import functools

import jax
import jax.numpy as jnp
from jax import lax
from jax.experimental import pallas as pl
from jax.experimental.pallas import tpu as pltpu
from jax.sharding import PartitionSpec as P

MESH = pl.DeviceIdType.MESH
F32 = jnp.float32
BF16 = jnp.bfloat16
CHUNKS = 4
ORDER = ((0, 1, 2, 3), (2, 3, 0, 1))


def kernel(
    n_row,
    n_grp,
    ints_ref,
    amps_ref,
    bases_ref,
    orbs_ref,
    count_ref,
    neigh_ref,
    coup_ref,
    occ_ref,
    virt_ref,
    out_ref,
    own,
    left1,
    left2,
    left3,
    right1,
    right2,
    right3,
    far,
    p_own,
    p_left1,
    p_left2,
    p_left3,
    p_right1,
    p_right2,
    p_right3,
    p_far,
    window,
    amp,
    base,
    local_sem,
    ring_send,
    ring_recv,
    core_send,
    core_recv,
    halo_send,
    halo_recv,
):
    row = lax.axis_index("row")
    grp = lax.axis_index("grp")
    slots = amp.shape[0]
    orbs = own.shape[0]
    size = orbs // CHUNKS
    ring_to = ((row + 2) % n_row, (row + n_row - 2) % n_row)
    partner = row + 1 - 2 * (row % 2)
    halo_to = ((grp + 1) % n_grp, (grp + n_grp - 1) % n_grp)

    loads = [
        pltpu.make_async_copy(src, dst, local_sem.at[i])
        for i, (src, dst) in enumerate(((ints_ref, own), (bases_ref, base), (amps_ref, amp)))
    ]
    for load in loads:
        load.start()

    barrier = pltpu.get_barrier_semaphore()
    peers = [(r, grp) for r in ring_to + (partner,)] + [(row, g) for g in halo_to]
    for peer in peers:
        pl.semaphore_signal(barrier, inc=1, device_id=peer, device_id_type=MESH)
    pl.semaphore_wait(barrier, len(peers))

    ring = ((own, left1, left2, left3), (own, right1, right2, right3))
    sends = []

    def ring_copy(way, step, chunk):
        src = ring[way][step]
        dst = ring[way][step + 1] if step < 3 else far
        part = pl.ds(chunk * size, size)
        return pltpu.make_async_remote_copy(
            src_ref=src.at[part],
            dst_ref=dst.at[part],
            send_sem=ring_send.at[way, step, chunk],
            recv_sem=ring_recv.at[way, step, chunk],
            device_id=(ring_to[way], grp),
            device_id_type=MESH,
        )

    pairs = (
        (own, p_own),
        (left1, p_left1),
        (right1, p_right1),
        (left2, p_left2),
        (right2, p_right2),
        (left3, p_left3),
        (right3, p_right3),
        (far, p_far),
    )
    place = (((1,), (3,), (5,), (7,)), ((2,), (4,), (6,), (7,)))

    def core_copy(which, chunk):
        src, dst = pairs[which]
        part = pl.ds(chunk * size, size)
        return pltpu.make_async_remote_copy(
            src_ref=src.at[part],
            dst_ref=dst.at[part],
            send_sem=core_send.at[which, chunk],
            recv_sem=core_recv.at[which, chunk],
            device_id=(partner, grp),
            device_id_type=MESH,
        )

    def halo_copy(way, slot):
        return pltpu.make_async_remote_copy(
            src_ref=window.at[slots + slot],
            dst_ref=window.at[(0 if way == 0 else 2 * slots) + slot],
            send_sem=halo_send.at[way, slot],
            recv_sem=halo_recv.at[way, slot],
            device_id=(row, halo_to[way]),
            device_id_type=MESH,
        )

    def start(copy):
        copy.start()
        sends.append(copy)

    loads[0].wait()
    for i in range(CHUNKS):
        for way in range(2):
            start(ring_copy(way, 0, ORDER[way][i]))
    for i in range(CHUNKS):
        start(core_copy(0, i))

    def dot(a, b, dims):
        return lax.dot_general(a, b, (dims, ((), ())), preferred_element_type=F32)

    count = count_ref[0, 0]
    alive = [jnp.where(s < count, 1.0, 0.0).astype(F32) for s in range(slots)]

    loads[1].wait()
    loads[2].wait()
    for s in range(slots):
        u = base[s]
        masked = (amp[s].astype(F32) * alive[s]).astype(BF16)
        first = dot(u, masked, ((1,), (0,))).astype(BF16)
        window[slots + s] = dot(first, u, ((1,), (1,))).astype(BF16)
        if s > 0:
            for way in range(2):
                start(halo_copy(way, s - 1))
    energy = jnp.transpose(virt_ref[...])
    for s in range(slots):
        denom = energy[:, s : s + 1] + virt_ref[s : s + 1, :] - occ_ref[s, 0]
        out_ref[s] = denom * amp[s].astype(F32)
        if s == 0:
            for way in range(2):
                start(halo_copy(way, slots - 1))

    def fock(buffers):
        lhs = jnp.concatenate([b[row] for b in buffers], axis=0).T
        for s in range(slots):
            other = orbs_ref[s, 1]
            rhs = jnp.concatenate([b[other] for b in buffers], axis=0)
            yield s, dot(lhs, rhs, ((1,), (0,)))

    def arrive(way, step, chunk, onward):
        ring_copy(way, step, chunk).wait_recv()
        if onward:
            start(ring_copy(way, step + 1, chunk))
        start(core_copy(place[way][step][0], chunk))

    def settle(which):
        for chunk in range(CHUNKS):
            core_copy(which, chunk).wait_recv()

    for i in range(CHUNKS):
        for way in range(2):
            arrive(way, 0, ORDER[way][i], True)
    settle(0)
    settle(1)
    settle(2)
    for s, term in fock((own, p_own, left1, p_left1)):
        out_ref[s] += term

    for i in range(CHUNKS):
        for way in range(2):
            arrive(way, 1, ORDER[way][i], True)
    settle(3)
    settle(4)
    for s, term in fock((right1, p_right1, left2, p_left2, right2, p_right2)):
        out_ref[s] += term

    for i in range(CHUNKS // 2):
        for way in range(2):
            arrive(way, 2, ORDER[way][i], True)

    for way in range(2):
        for s in range(slots):
            halo_copy(way, s).wait_recv()
    lowest = jnp.where(grp == 0, slots, 0)
    highest = jnp.where(grp == n_grp - 1, 2 * slots, 3 * slots)
    for s in range(slots):
        total = None
        for n in range(neigh_ref.shape[1]):
            at = neigh_ref[s, n]
            inside = jnp.logical_and(at >= lowest, at < highest)
            weight = jnp.where(inside, coup_ref[s, n], 0.0)
            term = weight * window[at].astype(F32)
            total = term if total is None else total + term
        u = base[s]
        back_first = dot(u.T, total.astype(BF16), ((1,), (0,))).astype(BF16)
        out_ref[s] -= dot(back_first, u, ((1,), (0,)))

    for i in range(CHUNKS // 2, CHUNKS):
        for way in range(2):
            arrive(way, 2, ORDER[way][i], False)
    settle(5)
    settle(6)
    for s, term in fock((left3, p_left3, right3, p_right3)):
        out_ref[s] += term

    for i in range(CHUNKS // 2):
        for way in range(2):
            arrive(way, 3, ORDER[way][i], False)
    settle(7)
    for s, term in fock((far, p_far)):
        out_ref[s] = (out_ref[s] + term) * alive[s]

    for copy in sends:
        copy.wait_send()


def solution(mesh):
    n_row, n_grp = mesh.shape["row"], mesh.shape["grp"]

    def local(ints, amps, orbs, count, neigh, coup, bases, virt, occ):
        slots = amps.shape[0]
        smem = pl.BlockSpec(memory_space=pltpu.SMEM)
        vmem = pl.BlockSpec(memory_space=pltpu.VMEM)
        hbm = pl.BlockSpec(memory_space=pl.ANY)
        return pl.pallas_call(
            functools.partial(kernel, n_row, n_grp),
            out_shape=jax.ShapeDtypeStruct(amps.shape, F32),
            in_specs=[hbm, hbm, hbm, smem, smem, smem, smem, smem, vmem],
            out_specs=vmem,
            scratch_shapes=[pltpu.VMEM(ints.shape, BF16)] * 16
            + [
                pltpu.VMEM((3 * slots,) + amps.shape[1:], BF16),
                pltpu.VMEM(amps.shape, BF16),
                pltpu.VMEM(amps.shape, BF16),
                pltpu.SemaphoreType.DMA((3,)),
                pltpu.SemaphoreType.DMA((2, 4, CHUNKS)),
                pltpu.SemaphoreType.DMA((2, 4, CHUNKS)),
                pltpu.SemaphoreType.DMA((8, CHUNKS)),
                pltpu.SemaphoreType.DMA((8, CHUNKS)),
                pltpu.SemaphoreType.DMA((2, slots)),
                pltpu.SemaphoreType.DMA((2, slots)),
            ],
            compiler_params=pltpu.CompilerParams(collective_id=0, has_side_effects=True),
        )(ints, amps, bases, orbs, count, neigh, coup, occ, virt)

    placed = (
        P("grp", "row", None),
        P("grp", "row", None),
        P("grp", "row"),
        P("grp", "row"),
        P("grp", "row"),
        P("grp", "row"),
        P("grp", "row", None),
        P("grp", "row"),
        P("grp", "row"),
    )
    return jax.shard_map(
        local, mesh=mesh, in_specs=placed, out_specs=P("grp", "row", None), check_vma=False
    )
```

time: 87.8 us -> 53.2 us (0.61)
  waiting for transfers between devices: 51.7 us -> 0 us
  Pallas kernels: 0 us -> 48.7 us
  between operations: 14.2 us -> 0.68 us
  matrix products: 8.51 us -> 0 us
  starting transfers between devices: 7.09 us -> 0 us
  local copies, waits for them, and re-layouts: 5.64 us -> 3.61 us
    pallas_call x0 -> x1, Pallas kernels: none -> 48.7 us  [local(): pl.pallas_call(functools.partial(kernel, n_row, n_grp), out_shape=jax.Sha...]
    all_gather x1 -> x0, waiting for transfers between devices: 41.1 us -> none  [local(): piece = lax.all_gather(integrals, 'row', axis=1, tiled=True)]
    ppermute x2 -> x0, waiting for transfers between devices: 9.98 us -> none  [the longest x1 5.36 us: with_halo(): after = lax.ppermute(initial, axis, down)]
    dot_general x4 -> x0, matrix products: 8.51 us -> none  [the longest x1 2.7 us: local(): jnp.einsum('pxa,pxb->pab', left, right, preferred_element_type=jnp.float32)]
    ppermute x2 -> x0, starting transfers between devices: 7.06 us -> none  [the longest x1 5.76 us: with_halo(): before = lax.ppermute(last, axis, up)]
    gather x2 -> x0, local copies, waits for them, and re-layouts: 5.61 us -> none  [the longest x1 2.81 us: local(): right = jnp.take(piece, second_orb, axis=0)]
    unnamed x12 -> x7, local copies, waits for them, and re-layouts: 0.03 us -> 3.61 us
  transfers between devices with their start and end apart: 3 -> 0, of which waited for: 3 -> 0; matrix products, arithmetic and copies ran while one was open for 4% -> 0% of each run, Pallas kernels for 0% -> 0%
where the time goes in v1:
time: 53.2 us; the launch traced here: 53 us
  Pallas kernels  48.7 us (92%)
  local copies, waits for them, and re-layouts  3.61 us (7%)
  between operations  0.68 us (1%)
    pallas_call x1, Pallas kernels, local(): pl.pallas_call(functools.partial(kernel, n_row, n_grp), out_shape=jax.Sha...  48.7 us
    unnamed x7, local copies, waits for them, and re-layouts  3.61 us

profile of v1, /device:TPU:1, one launch (start us, length us, event | category | flops | bytes accessed | tf_op | source)
XLA Modules:
  0.0 53.0 jit_solution(13912802752199574333)
XLA Ops:
  0.0 0.0 copy-start
  0.7 0.0 copy-done
  0.7 0.0 copy-start.1
  0.7 0.7 %copy.10.orbs_ref = s32[4,2]{1,0:T(4,128)} copy(s32[4,2]{0,1:T(2,128)S(1)} %copy-done) | data formatting | bytes 64 | tf_op args[2]
  1.4 0.0 copy-done.1
  1.4 0.6 %copy.11.occ_ref = f32[4,1]{1,0:T(4,128)} copy(f32[4,1]{0,1:T(1,128)S(1)} %copy-done.1) | data formatting | bytes 32 | tf_op args[8]
  2.0 48.7 %shard_map.91 = f32[4,256,256]{2,1,0:T(8,128)} custom-call(bf16[16,32,256]{2,1,0:T(8,128)(2,1)} %ints_ref.1, bf16[4,256,256]{2,1,0:T(8,128)(2,1)} %amps_ref.1, bf16[4,256,256]{2,1,0:T(8,128)(2,1)} %bases_ref.1, s32[4,2]{1,0:T(4,128)} %copy.10.orbs_ref, s32[1,1]{1,0:T(1,128)S(6)} %copy.13.count_ref, s32[4,4]{1,0:T(4,128)} %neigh_ref.1, f32[4,4]{1,0:T(4,128)} %coup_ref.1, ...), custom_call_target="tpu_custom_call" | custom-call | tf_op jit(solution)/shard_map/pallas_call | solution.py:246
  50.7 2.3 %copy.14 = f32[4,256,256]{2,1,0:T(8,128)} copy(f32[4,256,256]{2,1,0:T(8,128)} %shard_map.91) | data formatting | bytes 2097152
Async XLA Ops:
  0.0 0.7 %copy-start = (s32[4,2]{0,1:T(2,128)S(1)}, s32[4,2]{0,1:T(2,128)}, u32[]{:S(2)}) copy-start(s32[4,2]{0,1:T(2,128)} %param.11) | copy-start | bytes 100
  0.7 0.7 %copy-start.1 = (f32[4,1]{0,1:T(1,128)S(1)}, f32[4,1]{0,1:T(1,128)}, u32[]{:S(2)}) copy-start(f32[4,1]{0,1:T(1,128)} %param.17) | copy-start | bytes 52

commit v2 on v1

v2 whole, which is shorter than its diff:
```python
import functools

import jax
import jax.numpy as jnp
from jax import lax
from jax.experimental import pallas as pl
from jax.experimental.pallas import tpu as pltpu
from jax.sharding import PartitionSpec as P

MESH = pl.DeviceIdType.MESH
F32 = jnp.float32
BF16 = jnp.bfloat16
CHUNKS = 4
N_Z = 8
ORDER = ((0, 1, 2, 3), (2, 3, 0, 1))


def kernel(
    n_row,
    n_grp,
    ints_hbm,
    amps_hbm,
    bases_hbm,
    orbs_hbm,
    count_ref,
    neigh_hbm,
    coup_hbm,
    occ_hbm,
    virt_hbm,
    out_ref,
    own,
    left1,
    left2,
    left3,
    right1,
    right2,
    right3,
    far,
    p_own,
    p_left1,
    p_left2,
    p_left3,
    p_right1,
    p_right2,
    p_right3,
    p_far,
    window,
    amp,
    base,
    turned,
    orbs_ref,
    neigh_ref,
    coup_ref,
    occ_ref,
    virt_ref,
    local_sem,
    ring_send,
    ring_recv,
    core_send,
    core_recv,
    halo_send,
    halo_recv,
    ready,
):
    row = lax.axis_index("row")
    grp = lax.axis_index("grp")
    slots = amp.shape[0]
    orbs = own.shape[0]
    size = orbs // CHUNKS
    ring_to = ((row + 2) % n_row, (row + n_row - 2) % n_row)
    partner = row + 1 - 2 * (row % 2)
    halo_to = ((grp + 1) % n_grp, (grp + n_grp - 1) % n_grp)

    loads = [
        pltpu.make_async_copy(src, dst, local_sem.at[i])
        for i, (src, dst) in enumerate(
            (
                (bases_hbm, base),
                (amps_hbm, amp),
                (ints_hbm, own),
                (orbs_hbm, orbs_ref),
                (neigh_hbm, neigh_ref),
                (coup_hbm, coup_ref),
                (occ_hbm, occ_ref),
                (virt_hbm, virt_ref),
            )
        )
    ]
    for load in loads:
        load.start()

    core, z = row % 2, grp % N_Z
    has_up, has_down = grp < n_grp - 1, grp > 0
    up_first = jnp.logical_or(z == N_Z - 1, jnp.logical_and(row == 0, grp == 0))
    down_last = jnp.logical_or(z == 0, jnp.logical_and(row == 0, grp == 1))
    up_early = jnp.logical_and(has_up, up_first)
    up_late = jnp.logical_and(has_up, jnp.logical_not(up_first))
    down_late = jnp.logical_and(has_down, down_last)
    down_early = jnp.logical_and(has_down, jnp.logical_not(down_last))

    barrier = pltpu.get_barrier_semaphore()

    def signal(sem, r, g):
        pl.semaphore_signal(sem, inc=1, device_id=(r, g), device_id_type=MESH)

    for r in ring_to:
        signal(barrier, r, grp)
    pl.when(core == 1)(lambda: signal(barrier, partner, grp))
    pl.when(up_late)(lambda: signal(barrier, row, halo_to[0]))
    pl.when(down_late)(lambda: signal(barrier, row, halo_to[1]))
    pl.semaphore_wait(
        barrier,
        2 + (1 - core) + jnp.where(up_early, 1, 0) + jnp.where(down_early, 1, 0),
    )
    pl.when(core == 0)(lambda: signal(ready.at[2], partner, grp))
    pl.when(up_early)(lambda: signal(ready.at[1], row, halo_to[0]))
    pl.when(down_early)(lambda: signal(ready.at[0], row, halo_to[1]))

    ring = ((own, left1, left2, left3), (own, right1, right2, right3))
    sends = []

    def ring_copy(way, step, chunk):
        src = ring[way][step]
        dst = ring[way][step + 1] if step < 3 else far
        part = pl.ds(chunk * size, size)
        return pltpu.make_async_remote_copy(
            src_ref=src.at[part],
            dst_ref=dst.at[part],
            send_sem=ring_send.at[way, step, chunk],
            recv_sem=ring_recv.at[way, step, chunk],
            device_id=(ring_to[way], grp),
            device_id_type=MESH,
        )

    pairs = (
        (own, p_own),
        (left1, p_left1),
        (right1, p_right1),
        (left2, p_left2),
        (right2, p_right2),
        (left3, p_left3),
        (right3, p_right3),
        (far, p_far),
    )
    place = ((1, 3, 5, 7), (2, 4, 6, 7))

    def core_copy(which, chunk):
        src, dst = pairs[which]
        part = pl.ds(chunk * size, size)
        return pltpu.make_async_remote_copy(
            src_ref=src.at[part],
            dst_ref=dst.at[part],
            send_sem=core_send.at[which, chunk],
            recv_sem=core_recv.at[which, chunk],
            device_id=(partner, grp),
            device_id_type=MESH,
        )

    def halo_copy(way, slot):
        return pltpu.make_async_remote_copy(
            src_ref=window.at[slots + slot],
            dst_ref=window.at[(0 if way == 0 else 2 * slots) + slot],
            send_sem=halo_send.at[way, slot],
            recv_sem=halo_recv.at[way, slot],
            device_id=(row, halo_to[way]),
            device_id_type=MESH,
        )

    def start(copy):
        copy.start()
        sends.append(copy)

    loads[2].wait()
    for i in range(CHUNKS):
        for way in range(2):
            start(ring_copy(way, 0, ORDER[way][i]))
    def dot(a, b, dims):
        return lax.dot_general(a, b, (dims, ((), ())), preferred_element_type=F32)

    for load in loads[:2] + loads[3:]:
        load.wait()
    count = count_ref[0, 0]
    alive = [jnp.where(s < count, 1.0, 0.0).astype(F32) for s in range(slots)]

    def send_halo(way, tiles):
        for s in tiles:
            halo_copy(way, s).start()

    for s in range(slots):
        u = base[s]
        masked = (amp[s].astype(F32) * alive[s]).astype(BF16)
        first = dot(u, masked, ((1,), (0,))).astype(BF16)
        window[slots + s] = dot(first, u, ((1,), (1,))).astype(BF16)
        if s > 0:
            pl.when(up_early)(functools.partial(send_halo, 0, (s - 1,)))
            pl.when(down_early)(functools.partial(send_halo, 1, (s - 1,)))
    turned[0] = base[0].T
    pl.when(up_early)(functools.partial(send_halo, 0, (slots - 1,)))
    pl.when(down_early)(functools.partial(send_halo, 1, (slots - 1,)))

    @pl.when(up_late)
    def _():
        pl.semaphore_wait(ready.at[0], 1)
        send_halo(0, range(slots))

    for s in range(1, slots):
        turned[s] = base[s].T
    energy = jnp.transpose(virt_ref[...])
    for s in range(slots):
        denom = energy[:, s : s + 1] + virt_ref[s : s + 1, :] - occ_ref[0, s]
        out_ref[s] = denom * amp[s].astype(F32)

    @pl.when(grp == 0)
    def _():
        window[:slots] = jnp.zeros((slots,) + window.shape[1:], BF16)

    @pl.when(grp == n_grp - 1)
    def _():
        window[2 * slots :] = jnp.zeros((slots,) + window.shape[1:], BF16)

    def fock(buffers):
        lhs = jnp.concatenate([b[row] for b in buffers], axis=0).T
        for s in range(slots):
            other = orbs_ref[1, s]
            rhs = jnp.concatenate([b[other] for b in buffers], axis=0)
            out_ref[s] += dot(lhs, rhs, ((1,), (0,)))

    def arrive(way, step, chunk, onward):
        ring_copy(way, step, chunk).wait_recv()
        if onward:
            start(ring_copy(way, step + 1, chunk))

    def share(way, step, chunk):
        start(core_copy(place[way][step], chunk))

    def settle(which):
        for chunk in range(CHUNKS):
            core_copy(which, chunk).wait_recv()

    for step in range(2):
        for i in range(CHUNKS):
            for way in range(2):
                arrive(way, step, ORDER[way][i], True)
    fock((own, left1, right1, left2, right2))
    for i in range(CHUNKS // 2):
        for way in range(2):
            arrive(way, 2, ORDER[way][i], True)

    pl.when(core == 1)(lambda: pl.semaphore_wait(ready.at[2], 1))
    for which in range(5):
        for chunk in range(CHUNKS):
            start(core_copy(which, chunk))
    for i in range(CHUNKS // 2):
        for way in range(2):
            share(way, 2, ORDER[way][i])

    @pl.when(down_late)
    def _():
        pl.semaphore_wait(ready.at[1], 1)
        send_halo(1, range(slots))

    for i in range(CHUNKS // 2, CHUNKS):
        for way in range(2):
            arrive(way, 2, ORDER[way][i], False)
            share(way, 2, ORDER[way][i])
    for which in range(5):
        settle(which)
    fock((p_own, p_left1, p_right1, p_left2, p_right2, left3, right3))
    for i in range(CHUNKS // 2):
        for way in range(2):
            arrive(way, 3, ORDER[way][i], False)
            share(way, 3, ORDER[way][i])
    for which in range(5, 8):
        settle(which)
    fock((far, p_far, p_left3, p_right3))

    def take_halo(way):
        for s in range(slots):
            halo_copy(way, s).wait_recv()

    pl.when(has_up)(functools.partial(take_halo, 1))
    pl.when(has_down)(functools.partial(take_halo, 0))
    for s in range(slots):
        total = None
        for n in range(neigh_ref.shape[1]):
            term = coup_ref[s, n] * window[neigh_ref[s, n]].astype(F32)
            total = term if total is None else total + term
        back_first = dot(turned[s], total.astype(BF16), ((1,), (0,))).astype(BF16)
        back = dot(back_first, base[s], ((1,), (0,)))
        out_ref[s] = (out_ref[s] - back) * alive[s]

    for copy in sends:
        copy.wait_send()

    def sent_halo(way):
        for s in range(slots):
            halo_copy(way, s).wait_send()

    pl.when(has_up)(functools.partial(sent_halo, 0))
    pl.when(has_down)(functools.partial(sent_halo, 1))


def solution(mesh):
    n_row, n_grp = mesh.shape["row"], mesh.shape["grp"]

    def local(ints, amps, orbs, count, neigh, coup, bases, virt, occ):
        slots = amps.shape[0]
        args = (ints, amps, bases, orbs.T, count, neigh, coup, occ.T, virt)
        args = [a if a is count else pltpu.with_memory_space_constraint(a, pltpu.HBM) for a in args]
        return pl.pallas_call(
            functools.partial(kernel, n_row, n_grp),
            out_shape=jax.ShapeDtypeStruct(amps.shape, F32),
            in_specs=[
                pl.BlockSpec(memory_space=pltpu.SMEM if a is count else pl.ANY) for a in args
            ],
            out_specs=pl.BlockSpec(memory_space=pltpu.VMEM),
            scratch_shapes=[pltpu.VMEM(ints.shape, BF16)] * 16
            + [
                pltpu.VMEM((3 * slots,) + amps.shape[1:], BF16),
                pltpu.VMEM(amps.shape, BF16),
                pltpu.VMEM(amps.shape, BF16),
                pltpu.VMEM(amps.shape, BF16),
            ]
            + [pltpu.SMEM(a.shape, a.dtype) for a in (args[3],) + tuple(args[5:8])]
            + [
                pltpu.VMEM(virt.shape, F32),
                pltpu.SemaphoreType.DMA((len(args) - 1,)),
                pltpu.SemaphoreType.DMA((2, 4, CHUNKS)),
                pltpu.SemaphoreType.DMA((2, 4, CHUNKS)),
                pltpu.SemaphoreType.DMA((8, CHUNKS)),
                pltpu.SemaphoreType.DMA((8, CHUNKS)),
                pltpu.SemaphoreType.DMA((2, slots)),
                pltpu.SemaphoreType.DMA((2, slots)),
                pltpu.SemaphoreType.REGULAR((3,)),
            ],
            compiler_params=pltpu.CompilerParams(
                collective_id=0, has_side_effects=True, vmem_limit_bytes=16 << 20
            ),
        )(*args)

    placed = (
        P("grp", "row", None),
        P("grp", "row", None),
        P("grp", "row"),
        P("grp", "row"),
        P("grp", "row"),
        P("grp", "row"),
        P("grp", "row", None),
        P("grp", "row"),
        P("grp", "row"),
    )
    return jax.shard_map(
        local, mesh=mesh, in_specs=placed, out_specs=P("grp", "row", None), check_vma=False
    )
```

time: 53.2 us -> 37.4 us (0.70)
  Pallas kernels: 48.7 us -> 35.6 us
  local copies, waits for them, and re-layouts: 3.61 us -> 0.97 us
    pallas_call x1, Pallas kernels: 48.7 us -> 35.6 us  [local(): pl.pallas_call(functools.partial(kernel, n_row, n_grp), out_shape=jax.Sha...]
    unnamed x7 -> x1, local copies, waits for them, and re-layouts: 3.61 us -> 0.97 us
where the time goes in v2:
time: 37.4 us; the launch traced here: 37.2 us
  Pallas kernels  35.6 us (95%)
  local copies, waits for them, and re-layouts  0.97 us (3%)
  between operations  0.66 us (2%)
    pallas_call x1, Pallas kernels, local(): pl.pallas_call(functools.partial(kernel, n_row, n_grp), out_shape=jax.Sha...  35.6 us
    unnamed x1, local copies, waits for them, and re-layouts  0.97 us

profile of v2, /device:TPU:1, one launch (start us, length us, event | category | flops | bytes accessed | tf_op | source)
XLA Modules:
  0.0 37.2 jit_solution(13623081616825154950)
XLA Ops:
  0.7 35.6 %shard_map.91 = f32[4,256,256]{2,1,0:T(8,128)S(1)} custom-call(bf16[16,32,256]{2,1,0:T(8,128)(2,1)} %ints_hbm.1, bf16[4,256,256]{2,1,0:T(8,128)(2,1)} %amps_hbm.1, bf16[4,256,256]{2,1,0:T(8,128)(2,1)} %bases_hbm.1, s32[2,4]{1,0:T(2,128)} %bitcast.2, s32[1,1]{1,0:T(1,128)S(6)} %copy.11.count_ref, s32[4,4]{1,0:T(4,128)} %neigh_hbm.1, f32[4,4]{1,0:T(4,128)} %coup_hbm.1, ...), custom_call_target="tpu_custom_call" | custom-call | tf_op jit(solution)/shard_map/pallas_call | solution.py:310
  36.3 1.0 %copy.12 = f32[4,256,256]{2,1,0:T(8,128)} copy(f32[4,256,256]{2,1,0:T(8,128)S(1)} %shard_map.91) | data formatting | bytes 2097152

commit v3 on v2

v3 whole, which is shorter than its diff:
```python
import functools

import jax
import jax.numpy as jnp
from jax import lax
from jax.experimental import pallas as pl
from jax.experimental.pallas import tpu as pltpu
from jax.sharding import PartitionSpec as P

MESH = pl.DeviceIdType.MESH
F32 = jnp.float32
BF16 = jnp.bfloat16
CHUNKS = 4
N_Z = 8
ORDER = ((0, 1, 2, 3), (2, 3, 0, 1))


def kernel(
    n_row,
    n_grp,
    ints_hbm,
    amps_hbm,
    bases_hbm,
    orbs_hbm,
    count_ref,
    neigh_hbm,
    coup_hbm,
    occ_hbm,
    virt_hbm,
    out_ref,
    own,
    left1,
    left2,
    left3,
    right1,
    right2,
    right3,
    far,
    p_own,
    p_left1,
    p_left2,
    p_left3,
    p_right1,
    p_right2,
    p_right3,
    p_far,
    window,
    amp,
    base,
    turned,
    orbs_ref,
    neigh_ref,
    coup_ref,
    occ_ref,
    virt_ref,
    local_sem,
    ring_send,
    ring_recv,
    core_send,
    core_recv,
    halo_send,
    halo_recv,
    ready,
):
    row = lax.axis_index("row")
    grp = lax.axis_index("grp")
    slots = amp.shape[0]
    orbs = own.shape[0]
    size = orbs // CHUNKS
    ring_to = ((row + 2) % n_row, (row + n_row - 2) % n_row)
    partner = row + 1 - 2 * (row % 2)
    halo_to = ((grp + 1) % n_grp, (grp + n_grp - 1) % n_grp)

    loads = {}

    def load(name, src, dst):
        loads[name] = pltpu.make_async_copy(src, dst, local_sem.at[len(loads)])
        loads[name].start()

    for s in range(slots):
        load(f"base{s}", bases_hbm.at[s], base.at[s])
        load(f"amp{s}", amps_hbm.at[s], amp.at[s])
        if s == 0:
            load("own", ints_hbm, own)
    load("orbs", orbs_hbm, orbs_ref)
    load("neigh", neigh_hbm, neigh_ref)
    load("coup", coup_hbm, coup_ref)
    load("occ", occ_hbm, occ_ref)
    load("virt", virt_hbm, virt_ref)

    core, z = row % 2, grp % N_Z
    has_up, has_down = grp < n_grp - 1, grp > 0
    up_first = jnp.logical_or(z == N_Z - 1, jnp.logical_and(row == 0, grp == 0))
    down_last = jnp.logical_or(z == 0, jnp.logical_and(row == 0, grp == 1))
    up_early = jnp.logical_and(has_up, up_first)
    up_late = jnp.logical_and(has_up, jnp.logical_not(up_first))
    down_late = jnp.logical_and(has_down, down_last)
    down_early = jnp.logical_and(has_down, jnp.logical_not(down_last))
    n_x, x = n_row // 2, row // 2
    first_group = grp == 0
    both = jnp.logical_and(first_group, core == 1)
    none = jnp.logical_and(first_group, core == 0)
    carry = jnp.logical_not(none)

    barrier = pltpu.get_barrier_semaphore()

    def signal(sem, r, g):
        pl.semaphore_signal(sem, inc=1, device_id=(r, g), device_id_type=MESH)

    @pl.when(carry)
    def _():
        for r in ring_to:
            signal(barrier, r, grp)

    pl.when(core == 1)(lambda: signal(barrier, partner, grp))
    pl.when(up_late)(lambda: signal(barrier, row, halo_to[0]))
    pl.when(down_late)(lambda: signal(barrier, row, halo_to[1]))
    def dot(a, b, dims):
        return lax.dot_general(a, b, (dims, ((), ())), preferred_element_type=F32)

    alive = [jnp.where(s < count_ref[0, 0], 1.0, 0.0).astype(F32) for s in range(slots)]

    def move(s):
        loads[f"base{s}"].wait()
        loads[f"amp{s}"].wait()
        u = base[s]
        masked = (amp[s].astype(F32) * alive[s]).astype(BF16)
        first = dot(u, masked, ((1,), (0,))).astype(BF16)
        window[slots + s] = dot(first, u, ((1,), (1,))).astype(BF16)

    move(0)
    move(1)
    pl.semaphore_wait(
        barrier,
        jnp.where(carry, 2, 0)
        + (1 - core)
        + jnp.where(up_early, 1, 0)
        + jnp.where(down_early, 1, 0),
    )
    pl.when(core == 0)(lambda: signal(ready.at[2], partner, grp))
    pl.when(up_early)(lambda: signal(ready.at[1], row, halo_to[0]))
    pl.when(down_early)(lambda: signal(ready.at[0], row, halo_to[1]))

    left = ((own, left1, left2, left3, far), (p_own, p_left1, p_left2, p_left3, p_far))
    right = ((own, right1, right2, right3, far), (p_own, p_right1, p_right2, p_right3, p_far))
    ring = (left, right)
    held = (
        (own, left1, right1, left2, right2, left3, right3, far),
        (p_own, p_left1, p_right1, p_left2, p_right2, p_left3, p_right3, p_far),
    )
    place = ((1, 3, 5, 7), (2, 4, 6, 7))

    def ring_copy(lane, way, step, chunk):
        part = pl.ds(chunk * size, size)
        return pltpu.make_async_remote_copy(
            src_ref=ring[way][lane][step].at[part],
            dst_ref=ring[way][lane][step + 1].at[part],
            send_sem=ring_send.at[lane, way, step, chunk],
            recv_sem=ring_recv.at[lane, way, step, chunk],
            device_id=(ring_to[way], grp),
            device_id_type=MESH,
        )

    def core_copy(lane, which, chunk):
        part = pl.ds(chunk * size, size)
        return pltpu.make_async_remote_copy(
            src_ref=held[lane][which].at[part],
            dst_ref=held[1 - lane][which].at[part],
            send_sem=core_send.at[lane, which, chunk],
            recv_sem=core_recv.at[lane, which, chunk],
            device_id=(partner, grp),
            device_id_type=MESH,
        )

    def halo_copy(way, slot):
        return pltpu.make_async_remote_copy(
            src_ref=window.at[slots + slot],
            dst_ref=window.at[(0 if way == 0 else 2 * slots) + slot],
            send_sem=halo_send.at[way, slot],
            recv_sem=halo_recv.at[way, slot],
            device_id=(row, halo_to[way]),
            device_id_type=MESH,
        )

    def send_halo(way, tiles):
        for s in tiles:
            halo_copy(way, s).start()

    def send_early(tiles):
        pl.when(up_early)(functools.partial(send_halo, 0, tiles))
        pl.when(down_early)(functools.partial(send_halo, 1, tiles))

    def set_out(lane):
        for i in range(CHUNKS):
            for way in range(2):
                ring_copy(lane, way, 0, ORDER[way][i]).start()

    loads["own"].wait()
    send_early((0,))
    pl.when(carry)(functools.partial(set_out, 0))

    @pl.when(none)
    def _():
        for chunk in range(CHUNKS):
            core_copy(0, 0, chunk).start()

    send_early((1,))
    move(2)
    move(3)
    turned[0] = base[0].T
    send_early((2, 3))

    def settle(lane, which):
        for chunk in range(CHUNKS):
            core_copy(lane, which, chunk).wait_recv()

    @pl.when(jnp.logical_and(both, x > 0))
    def _():
        settle(0, 0)
        set_out(1)

    @pl.when(up_late)
    def _():
        pl.semaphore_wait(ready.at[0], 1)
        send_halo(0, range(slots))

    for s in range(1, slots):
        turned[s] = base[s].T
    for name in ("orbs", "neigh", "coup", "occ", "virt"):
        loads[name].wait()
    energy = jnp.transpose(virt_ref[...])
    for s in range(slots):
        denom = energy[:, s : s + 1] + virt_ref[s : s + 1, :] - occ_ref[0, s]
        out_ref[s] = denom * amp[s].astype(F32)

    @pl.when(grp == 0)
    def _():
        window[:slots] = jnp.zeros((slots,) + window.shape[1:], BF16)

    @pl.when(grp == n_grp - 1)
    def _():
        window[2 * slots :] = jnp.zeros((slots,) + window.shape[1:], BF16)

    def fock(buffers):
        lhs = jnp.concatenate([b[row] for b in buffers], axis=0).T
        for s in range(slots):
            other = orbs_ref[1, s]
            rhs = jnp.concatenate([b[other] for b in buffers], axis=0)
            out_ref[s] += dot(lhs, rhs, ((1,), (0,)))

    def arrive(lane, way, step, chunk):
        ring_copy(lane, way, step, chunk).wait_recv()
        if step < 2 or (step == 2 and chunk in ORDER[way][: CHUNKS // 2]):
            ring_copy(lane, way, step + 1, chunk).start()

    def share(lane, way, step, chunk):
        core_copy(lane, place[way][step], chunk).start()

    def late(way, step):
        return jnp.logical_and(both, x == (step + 1 if way == 0 else n_x - 1 - step))

    def on_time(way, step):
        return jnp.logical_and(both, x != (step + 1 if way == 0 else n_x - 1 - step))

    def chunks(way, step):
        return ORDER[way][: CHUNKS if step < 3 else CHUNKS // 2]

    def each(step, part, *acts):
        for i in part:
            for way in range(2):

                @pl.when(carry)
                def _():
                    for act in acts:
                        act(0, way, step, ORDER[way][i])

                @pl.when(on_time(way, step))
                def _():
                    for act in acts:
                        act(1, way, step, ORDER[way][i])

    half, whole = range(CHUNKS // 2), range(CHUNKS)
    rest = range(CHUNKS // 2, CHUNKS)
    each(0, whole, arrive)
    each(1, whole, arrive)
    near = (own, left1, right1, left2, right2)
    pl.when(carry)(lambda: fock(near))
    each(2, half, arrive)

    pl.when(core == 1)(lambda: pl.semaphore_wait(ready.at[2], 1))

    @pl.when(carry)
    def _():
        for chunk in whole:
            core_copy(0, 0, chunk).start()

    each(0, whole, share)
    each(1, whole, share)
    each(2, half, share)

    @pl.when(down_late)
    def _():
        pl.semaphore_wait(ready.at[1], 1)
        send_halo(1, range(slots))

    each(2, rest, arrive, share)

    def settle_all(lane, which):
        for w in which:
            settle(lane, w)

    other = (p_own, p_left1, p_right1, p_left2, p_right2, left3, right3)

    @pl.when(jnp.logical_not(first_group))
    def _():
        settle_all(0, range(5))
        fock(other)

    each(3, half, arrive, share)

    @pl.when(jnp.logical_not(first_group))
    def _():
        settle_all(0, range(5, 8))

    @pl.when(jnp.logical_and(both, x == 0))
    def _():
        settle(0, 0)
        set_out(1)

    for step in range(4):
        for way in range(2):

            @pl.when(late(way, step))
            def _():
                for chunk in chunks(way, step):
                    arrive(1, way, step, chunk)
                    share(1, way, step, chunk)

    @pl.when(none)
    def _():
        settle_all(0, range(8))
        settle_all(1, range(1, 8))
        fock(near)

    pl.when(first_group)(lambda: fock(other))
    fock((far, p_far, p_left3, p_right3))

    def take_halo(way):
        for s in range(slots):
            halo_copy(way, s).wait_recv()

    pl.when(has_up)(functools.partial(take_halo, 1))
    pl.when(has_down)(functools.partial(take_halo, 0))
    for s in range(slots):
        total = None
        for n in range(neigh_ref.shape[1]):
            term = coup_ref[s, n] * window[neigh_ref[s, n]].astype(F32)
            total = term if total is None else total + term
        back_first = dot(turned[s], total.astype(BF16), ((1,), (0,))).astype(BF16)
        back = dot(back_first, base[s], ((1,), (0,)))
        out_ref[s] = (out_ref[s] - back) * alive[s]

    def sent(lane):
        for way in range(2):
            for step in range(4):
                for chunk in chunks(way, step):
                    ring_copy(lane, way, step, chunk).wait_send()
        for which in range(lane, len(held[lane])):
            for chunk in whole:
                core_copy(lane, which, chunk).wait_send()

    pl.when(carry)(functools.partial(sent, 0))
    pl.when(both)(functools.partial(sent, 1))

    @pl.when(none)
    def _():
        for chunk in whole:
            core_copy(0, 0, chunk).wait_send()

    def sent_halo(way):
        for s in range(slots):
            halo_copy(way, s).wait_send()

    pl.when(has_up)(functools.partial(sent_halo, 0))
    pl.when(has_down)(functools.partial(sent_halo, 1))


def solution(mesh):
    n_row, n_grp = mesh.shape["row"], mesh.shape["grp"]

    def local(ints, amps, orbs, count, neigh, coup, bases, virt, occ):
        slots = amps.shape[0]
        args = (ints, amps, bases, orbs.T, count, neigh, coup, occ.T, virt)
        args = [a if a is count else pltpu.with_memory_space_constraint(a, pltpu.HBM) for a in args]
        return pl.pallas_call(
            functools.partial(kernel, n_row, n_grp),
            out_shape=jax.ShapeDtypeStruct(amps.shape, F32),
            in_specs=[
                pl.BlockSpec(memory_space=pltpu.SMEM if a is count else pl.ANY) for a in args
            ],
            out_specs=pl.BlockSpec(memory_space=pltpu.VMEM),
            scratch_shapes=[pltpu.VMEM(ints.shape, BF16)] * 16
            + [
                pltpu.VMEM((3 * slots,) + amps.shape[1:], BF16),
                pltpu.VMEM(amps.shape, BF16),
                pltpu.VMEM(amps.shape, BF16),
                pltpu.VMEM(amps.shape, BF16),
            ]
            + [pltpu.SMEM(a.shape, a.dtype) for a in (args[3],) + tuple(args[5:8])]
            + [
                pltpu.VMEM(virt.shape, F32),
                pltpu.SemaphoreType.DMA((2 * slots + 6,)),
                pltpu.SemaphoreType.DMA((2, 2, 4, CHUNKS)),
                pltpu.SemaphoreType.DMA((2, 2, 4, CHUNKS)),
                pltpu.SemaphoreType.DMA((2, 8, CHUNKS)),
                pltpu.SemaphoreType.DMA((2, 8, CHUNKS)),
                pltpu.SemaphoreType.DMA((2, slots)),
                pltpu.SemaphoreType.DMA((2, slots)),
                pltpu.SemaphoreType.REGULAR((3,)),
            ],
            compiler_params=pltpu.CompilerParams(
                collective_id=0, has_side_effects=True, vmem_limit_bytes=16 << 20
            ),
        )(*args)

    placed = (
        P("grp", "row", None),
        P("grp", "row", None),
        P("grp", "row"),
        P("grp", "row"),
        P("grp", "row"),
        P("grp", "row"),
        P("grp", "row", None),
        P("grp", "row"),
        P("grp", "row"),
    )
    return jax.shard_map(
        local, mesh=mesh, in_specs=placed, out_specs=P("grp", "row", None), check_vma=False
    )
```

time: 37.4 us -> 40.9 us (1.094)
  the two profiles are of different devices: /device:TPU:1 before, /device:TPU:8 now
where the time goes in v3:
time: 40.9 us; the launch traced here: 40.8 us
  Pallas kernels  39.1 us (96%)
  local copies, waits for them, and re-layouts  0.97 us (2%)
  between operations  0.66 us (2%)
    pallas_call x1, Pallas kernels, local(): pl.pallas_call(functools.partial(kernel, n_row, n_grp), out_shape=jax.Sha...  39.1 us
    unnamed x1, local copies, waits for them, and re-layouts  0.97 us

profile of v3, /device:TPU:8, one launch (start us, length us, event | category | flops | bytes accessed | tf_op | source)
XLA Modules:
  0.0 40.8 jit_solution(3800976130561681325)
XLA Ops:
  0.7 39.1 %shard_map.91 = f32[4,256,256]{2,1,0:T(8,128)S(1)} custom-call(bf16[16,32,256]{2,1,0:T(8,128)(2,1)} %ints_hbm.1, bf16[4,256,256]{2,1,0:T(8,128)(2,1)} %amps_hbm.1, bf16[4,256,256]{2,1,0:T(8,128)(2,1)} %bases_hbm.1, s32[2,4]{1,0:T(2,128)} %bitcast.2, s32[1,1]{1,0:T(1,128)S(6)} %copy.11.count_ref, s32[4,4]{1,0:T(4,128)} %neigh_hbm.1, f32[4,4]{1,0:T(4,128)} %coup_hbm.1, ...), custom_call_target="tpu_custom_call" | custom-call | tf_op jit(solution)/shard_map/pallas_call | solution.py:395
  39.8 1.0 %copy.12 = f32[4,256,256]{2,1,0:T(8,128)} copy(f32[4,256,256]{2,1,0:T(8,128)S(1)} %shard_map.91) | data formatting | bytes 2097152

commit v4 on v2

v4 whole, which is shorter than its diff:
```python
import functools

import jax
import jax.numpy as jnp
from jax import lax
from jax.experimental import pallas as pl
from jax.experimental.pallas import tpu as pltpu
from jax.sharding import PartitionSpec as P

MESH = pl.DeviceIdType.MESH
F32 = jnp.float32
BF16 = jnp.bfloat16
CHUNKS = 4
N_Z = 8
ORDER = ((0, 1, 2, 3), (2, 3, 0, 1))


def kernel(
    n_row,
    n_grp,
    ints_hbm,
    amps_hbm,
    bases_hbm,
    orbs_hbm,
    count_ref,
    neigh_hbm,
    coup_hbm,
    occ_hbm,
    virt_hbm,
    out_ref,
    own,
    left1,
    left2,
    left3,
    right1,
    right2,
    right3,
    far,
    p_own,
    p_left1,
    p_left2,
    p_left3,
    p_right1,
    p_right2,
    p_right3,
    p_far,
    window,
    amp,
    base,
    turned,
    orbs_ref,
    neigh_ref,
    coup_ref,
    occ_ref,
    virt_ref,
    local_sem,
    ring_send,
    ring_recv,
    core_send,
    core_recv,
    halo_send,
    halo_recv,
    ready,
):
    row = lax.axis_index("row")
    grp = lax.axis_index("grp")
    slots = amp.shape[0]
    orbs = own.shape[0]
    size = orbs // CHUNKS
    ring_to = ((row + 2) % n_row, (row + n_row - 2) % n_row)
    partner = row + 1 - 2 * (row % 2)
    halo_to = ((grp + 1) % n_grp, (grp + n_grp - 1) % n_grp)

    loads = {}

    def load(name, src, dst):
        loads[name] = pltpu.make_async_copy(src, dst, local_sem.at[len(loads)])
        loads[name].start()

    for s in range(slots):
        load(f"base{s}", bases_hbm.at[s], base.at[s])
        load(f"amp{s}", amps_hbm.at[s], amp.at[s])
        if s == 0:
            load("own", ints_hbm, own)
    load("orbs", orbs_hbm, orbs_ref)
    load("neigh", neigh_hbm, neigh_ref)
    load("coup", coup_hbm, coup_ref)
    load("occ", occ_hbm, occ_ref)
    load("virt", virt_hbm, virt_ref)

    core, z = row % 2, grp % N_Z
    has_up, has_down = grp < n_grp - 1, grp > 0
    up_first = jnp.logical_or(z == N_Z - 1, jnp.logical_and(row == 0, grp == 0))
    down_last = jnp.logical_or(z == 0, jnp.logical_and(row == 0, grp == 1))
    up_early = jnp.logical_and(has_up, up_first)
    up_late = jnp.logical_and(has_up, jnp.logical_not(up_first))
    down_late = jnp.logical_and(has_down, down_last)
    down_early = jnp.logical_and(has_down, jnp.logical_not(down_last))
    n_x, x = n_row // 2, row // 2
    first = jnp.logical_and(row == 0, grp == 0)
    special = jnp.logical_and(jnp.logical_and(grp == 0, core == 0), x > 0)
    beside = jnp.logical_and(special, jnp.logical_or(x == 1, x == n_x - 1))

    barrier = pltpu.get_barrier_semaphore()

    def signal(sem, r, g):
        pl.semaphore_signal(sem, inc=1, device_id=(r, g), device_id_type=MESH)

    def greet(sem):
        for r in ring_to:
            signal(sem, r, grp)

    pl.when(jnp.logical_not(first))(lambda: greet(barrier))
    pl.when(core == 1)(lambda: signal(barrier, partner, grp))
    pl.when(up_late)(lambda: signal(barrier, row, halo_to[0]))
    pl.when(down_late)(lambda: signal(barrier, row, halo_to[1]))
    pl.semaphore_wait(
        barrier,
        jnp.where(beside, 1, 2)
        + (1 - core)
        + jnp.where(up_early, 1, 0)
        + jnp.where(down_early, 1, 0),
    )
    pl.when(first)(lambda: greet(ready.at[3]))
    pl.when(core == 0)(lambda: signal(ready.at[2], partner, grp))
    pl.when(up_early)(lambda: signal(ready.at[1], row, halo_to[0]))
    pl.when(down_early)(lambda: signal(ready.at[0], row, halo_to[1]))

    ring = ((own, left1, left2, left3, far), (own, right1, right2, right3, far))
    held = (
        (own, left1, right1, left2, right2, left3, right3, far),
        (p_own, p_left1, p_right1, p_left2, p_right2, p_left3, p_right3, p_far),
    )
    place = ((1, 3, 5, 7), (2, 4, 6, 7))

    def ring_copy(way, step, chunk):
        part = pl.ds(chunk * size, size)
        return pltpu.make_async_remote_copy(
            src_ref=ring[way][step].at[part],
            dst_ref=ring[way][step + 1].at[part],
            send_sem=ring_send.at[way, step, chunk],
            recv_sem=ring_recv.at[way, step, chunk],
            device_id=(ring_to[way], grp),
            device_id_type=MESH,
        )

    def core_copy(which, chunk):
        part = pl.ds(chunk * size, size)
        return pltpu.make_async_remote_copy(
            src_ref=held[0][which].at[part],
            dst_ref=held[1][which].at[part],
            send_sem=core_send.at[which, chunk],
            recv_sem=core_recv.at[which, chunk],
            device_id=(partner, grp),
            device_id_type=MESH,
        )

    def halo_copy(way, slot):
        return pltpu.make_async_remote_copy(
            src_ref=window.at[slots + slot],
            dst_ref=window.at[(0 if way == 0 else 2 * slots) + slot],
            send_sem=halo_send.at[way, slot],
            recv_sem=halo_recv.at[way, slot],
            device_id=(row, halo_to[way]),
            device_id_type=MESH,
        )

    def send_halo(way, tiles):
        for s in tiles:
            halo_copy(way, s).start()

    def send_early(tiles):
        pl.when(up_early)(functools.partial(send_halo, 0, tiles))
        pl.when(down_early)(functools.partial(send_halo, 1, tiles))

    def chunks(way, step):
        return ORDER[way][: CHUNKS if step < 3 else CHUNKS // 2]

    loads["own"].wait()

    @pl.when(jnp.logical_not(beside))
    def _():
        for i in range(CHUNKS):
            for way in range(2):
                ring_copy(way, 0, ORDER[way][i]).start()

    for way, away in enumerate((1, n_x - 1)):

        @pl.when(jnp.logical_and(beside, x == away))
        def _():
            for chunk in ORDER[way]:
                ring_copy(way, 0, chunk).start()

    def dot(a, b, dims):
        return lax.dot_general(a, b, (dims, ((), ())), preferred_element_type=F32)

    alive = [jnp.where(s < count_ref[0, 0], 1.0, 0.0).astype(F32) for s in range(slots)]
    for s in range(slots):
        loads[f"base{s}"].wait()
        loads[f"amp{s}"].wait()
        u = base[s]
        masked = (amp[s].astype(F32) * alive[s]).astype(BF16)
        mid = dot(u, masked, ((1,), (0,))).astype(BF16)
        window[slots + s] = dot(mid, u, ((1,), (1,))).astype(BF16)
        turned[s] = u.T
        send_early((s,))

    @pl.when(up_late)
    def _():
        pl.semaphore_wait(ready.at[0], 1)
        send_halo(0, range(slots))

    for name in ("orbs", "neigh", "coup", "occ", "virt"):
        loads[name].wait()
    energy = jnp.transpose(virt_ref[...])
    for s in range(slots):
        denom = energy[:, s : s + 1] + virt_ref[s : s + 1, :] - occ_ref[0, s]
        out_ref[s] = denom * amp[s].astype(F32)

    @pl.when(grp == 0)
    def _():
        window[:slots] = jnp.zeros((slots,) + window.shape[1:], BF16)

    @pl.when(grp == n_grp - 1)
    def _():
        window[2 * slots :] = jnp.zeros((slots,) + window.shape[1:], BF16)

    def fock(buffers):
        lhs = jnp.concatenate([b[row] for b in buffers], axis=0).T
        for s in range(slots):
            other = orbs_ref[1, s]
            rhs = jnp.concatenate([b[other] for b in buffers], axis=0)
            out_ref[s] += dot(lhs, rhs, ((1,), (0,)))

    half, whole, rest = range(CHUNKS // 2), range(CHUNKS), range(CHUNKS // 2, CHUNKS)
    near = (own, left1, right1, left2, right2)
    other = (p_own, p_left1, p_right1, p_left2, p_right2, left3, right3)
    last = (far, p_far, p_left3, p_right3)

    def forward(way, step, chunk):
        if step < 2 or (step == 2 and chunk in ORDER[way][: CHUNKS // 2]):
            ring_copy(way, step + 1, chunk).start()

    def arrive(way, step, chunk):
        ring_copy(way, step, chunk).wait_recv()
        forward(way, step, chunk)

    def share(way, step, chunk):
        core_copy(place[way][step], chunk).start()

    def share_all(which):
        for w in which:
            for chunk in whole:
                core_copy(w, chunk).start()

    def settle(which):
        for w in which:
            for chunk in whole:
                core_copy(w, chunk).wait_recv()

    def each(step, part, *acts):
        for i in part:
            for way in range(2):
                for act in acts:
                    act(way, step, ORDER[way][i])

    @pl.when(jnp.logical_not(special))
    def _():
        each(0, whole, arrive)
        each(1, whole, arrive)
        fock(near)
        each(2, half, arrive)
        pl.when(core == 1)(lambda: pl.semaphore_wait(ready.at[2], 1))
        share_all(range(5))
        each(2, half, share)

        @pl.when(down_late)
        def _():
            pl.semaphore_wait(ready.at[1], 1)
            send_halo(1, range(slots))

        each(2, rest, arrive, share)
        each(3, half, arrive, share)
        settle(range(5))
        fock(other)
        settle(range(5, 8))
        fock(last)

    def hops(way):
        return x if way == 0 else n_x - x

    @pl.when(special)
    def _():
        for step in range(4):
            for i in range(len(chunks(0, step))):
                for way in range(2):

                    @pl.when(hops(way) > step + 1)
                    def _():
                        ring_copy(way, step, ORDER[way][i]).wait_recv()
                        pl.when(hops(way) < n_x - 1)(
                            functools.partial(forward, way, step, ORDER[way][i])
                        )

        share_all((0,))
        for step in range(4):
            for way in range(2):

                @pl.when(hops(way) > step + 1)
                def _():
                    for chunk in chunks(way, step):
                        share(way, step, chunk)

        pl.when(beside)(lambda: pl.semaphore_wait(ready.at[3], 1))
        for way in range(2):

            @pl.when(hops(way) == n_x - 1)
            def _():
                for step in range(4):
                    for chunk in chunks(way, step):
                        ring_copy(way, step, chunk).start()

        for step in range(4):
            for way in range(2):

                @pl.when(hops(way) <= step + 1)
                def _():
                    for chunk in chunks(way, step):
                        arrive(way, step, chunk)
                        share(way, step, chunk)

        settle(range(8))
        fock(near)
        fock(other)
        fock(last)

    for way in range(2):
        for step in range(4):
            for chunk in chunks(way, step):
                ring_copy(way, step, chunk).wait_send()
    for which in range(8):
        for chunk in whole:
            core_copy(which, chunk).wait_send()

    def take_halo(way):
        for s in range(slots):
            halo_copy(way, s).wait_recv()

    pl.when(has_up)(functools.partial(take_halo, 1))
    pl.when(has_down)(functools.partial(take_halo, 0))
    for s in range(slots):
        total = None
        for n in range(neigh_ref.shape[1]):
            term = coup_ref[s, n] * window[neigh_ref[s, n]].astype(F32)
            total = term if total is None else total + term
        back_first = dot(turned[s], total.astype(BF16), ((1,), (0,))).astype(BF16)
        back = dot(back_first, base[s], ((1,), (0,)))
        out_ref[s] = (out_ref[s] - back) * alive[s]

    def sent_halo(way):
        for s in range(slots):
            halo_copy(way, s).wait_send()

    pl.when(has_up)(functools.partial(sent_halo, 0))
    pl.when(has_down)(functools.partial(sent_halo, 1))


def solution(mesh):
    n_row, n_grp = mesh.shape["row"], mesh.shape["grp"]

    def local(ints, amps, orbs, count, neigh, coup, bases, virt, occ):
        slots = amps.shape[0]
        args = (ints, amps, bases, orbs.T, count, neigh, coup, occ.T, virt)
        args = [a if a is count else pltpu.with_memory_space_constraint(a, pltpu.HBM) for a in args]
        return pl.pallas_call(
            functools.partial(kernel, n_row, n_grp),
            out_shape=jax.ShapeDtypeStruct(amps.shape, F32),
            in_specs=[
                pl.BlockSpec(memory_space=pltpu.SMEM if a is count else pl.ANY) for a in args
            ],
            out_specs=pl.BlockSpec(memory_space=pltpu.VMEM),
            scratch_shapes=[pltpu.VMEM(ints.shape, BF16)] * 16
            + [
                pltpu.VMEM((3 * slots,) + amps.shape[1:], BF16),
                pltpu.VMEM(amps.shape, BF16),
                pltpu.VMEM(amps.shape, BF16),
                pltpu.VMEM(amps.shape, BF16),
            ]
            + [pltpu.SMEM(a.shape, a.dtype) for a in (args[3],) + tuple(args[5:8])]
            + [
                pltpu.VMEM(virt.shape, F32),
                pltpu.SemaphoreType.DMA((2 * slots + 6,)),
                pltpu.SemaphoreType.DMA((2, 4, CHUNKS)),
                pltpu.SemaphoreType.DMA((2, 4, CHUNKS)),
                pltpu.SemaphoreType.DMA((8, CHUNKS)),
                pltpu.SemaphoreType.DMA((8, CHUNKS)),
                pltpu.SemaphoreType.DMA((2, slots)),
                pltpu.SemaphoreType.DMA((2, slots)),
                pltpu.SemaphoreType.REGULAR((4,)),
            ],
            compiler_params=pltpu.CompilerParams(
                collective_id=0, has_side_effects=True, vmem_limit_bytes=16 << 20
            ),
        )(*args)

    placed = (
        P("grp", "row", None),
        P("grp", "row", None),
        P("grp", "row"),
        P("grp", "row"),
        P("grp", "row"),
        P("grp", "row"),
        P("grp", "row", None),
        P("grp", "row"),
        P("grp", "row"),
    )
    return jax.shard_map(
        local, mesh=mesh, in_specs=placed, out_specs=P("grp", "row", None), check_vma=False
    )
```

time: 37.4 us -> 44.7 us (1.20)
  Pallas kernels: 35.6 us -> 42.9 us
    pallas_call x1, Pallas kernels: 35.6 us -> 42.9 us  [local(): pl.pallas_call(functools.partial(kernel, n_row, n_grp), out_shape=jax.Sha...]
where the time goes in v4:
time: 44.7 us; the launch traced here: 44.6 us
  Pallas kernels  42.9 us (96%)
  local copies, waits for them, and re-layouts  0.97 us (2%)
  between operations  0.66 us (1%)
    pallas_call x1, Pallas kernels, local(): pl.pallas_call(functools.partial(kernel, n_row, n_grp), out_shape=jax.Sha...  42.9 us
    unnamed x1, local copies, waits for them, and re-layouts  0.97 us

profile of v4, /device:TPU:1, one launch (start us, length us, event | category | flops | bytes accessed | tf_op | source)
XLA Modules:
  0.0 44.6 jit_solution(5281836178795829200)
XLA Ops:
  0.7 42.9 %shard_map.91 = f32[4,256,256]{2,1,0:T(8,128)S(1)} custom-call(bf16[16,32,256]{2,1,0:T(8,128)(2,1)} %ints_hbm.1, bf16[4,256,256]{2,1,0:T(8,128)(2,1)} %amps_hbm.1, bf16[4,256,256]{2,1,0:T(8,128)(2,1)} %bases_hbm.1, s32[2,4]{1,0:T(2,128)} %bitcast.2, s32[1,1]{1,0:T(1,128)S(6)} %copy.11.count_ref, s32[4,4]{1,0:T(4,128)} %neigh_hbm.1, f32[4,4]{1,0:T(4,128)} %coup_hbm.1, ...), custom_call_target="tpu_custom_call" | custom-call | tf_op jit(solution)/shard_map/pallas_call | solution.py:375
  43.6 1.0 %copy.12 = f32[4,256,256]{2,1,0:T(8,128)} copy(f32[4,256,256]{2,1,0:T(8,128)S(1)} %shard_map.91) | data formatting | bytes 2097152

commit v5 on v4

--- a/solution.py
+++ b/solution.py
@@ -58,6 +58,10 @@
     ring_recv,
     core_send,
     core_recv,
+    relay_send,
+    relay_recv,
+    back_send,
+    back_recv,
     halo_send,
     halo_recv,
     ready,
@@ -97,31 +101,45 @@
     down_late = jnp.logical_and(has_down, down_last)
     down_early = jnp.logical_and(has_down, jnp.logical_not(down_last))
     n_x, x = n_row // 2, row // 2
-    first = jnp.logical_and(row == 0, grp == 0)
-    special = jnp.logical_and(jnp.logical_and(grp == 0, core == 0), x > 0)
-    beside = jnp.logical_and(special, jnp.logical_or(x == 1, x == n_x - 1))
+    in_group = grp == 0
+    first = jnp.logical_and(row == 0, in_group)
+    relay = jnp.logical_and(row == 1, in_group)
+    special = jnp.logical_and(jnp.logical_and(in_group, core == 0), x > 0)
+    usual = jnp.logical_not(jnp.logical_or(special, jnp.logical_and(in_group, x == 0)))
+    odd = jnp.logical_and(special, x % 2 == 1)
 
     barrier = pltpu.get_barrier_semaphore()
 
     def signal(sem, r, g):
         pl.semaphore_signal(sem, inc=1, device_id=(r, g), device_id_type=MESH)
 
-    def greet(sem):
+    @pl.when(jnp.logical_not(jnp.logical_or(first, special)))
+    def _():
         for r in ring_to:
-            signal(sem, r, grp)
-
-    pl.when(jnp.logical_not(first))(lambda: greet(barrier))
+            signal(barrier, r, grp)
+
+    @pl.when(special)
+    def _():
+        for r in ring_to:
+            signal(barrier, jnp.where(r == 0, 1, r), grp)
+
+    pl.when(odd)(lambda: signal(barrier, 0, grp))
+
+    @pl.when(relay)
+    def _():
+        for r in (2, n_row - 2):
+            signal(barrier, r, grp)
+
     pl.when(core == 1)(lambda: signal(barrier, partner, grp))
     pl.when(up_late)(lambda: signal(barrier, row, halo_to[0]))
     pl.when(down_late)(lambda: signal(barrier, row, halo_to[1]))
     pl.semaphore_wait(
         barrier,
-        jnp.where(beside, 1, 2)
+        jnp.where(jnp.logical_or(first, relay), 4, 2)
         + (1 - core)
         + jnp.where(up_early, 1, 0)
         + jnp.where(down_early, 1, 0),
     )
-    pl.when(first)(lambda: greet(ready.at[3]))
     pl.when(core == 0)(lambda: signal(ready.at[2], partner, grp))
     pl.when(up_early)(lambda: signal(ready.at[1], row, halo_to[0]))
     pl.when(down_early)(lambda: signal(ready.at[0], row, halo_to[1]))
@@ -155,6 +173,62 @@
             device_id_type=MESH,
         )
 
+    other_ring = (
+        (p_own, p_left1, p_left2, p_left3, p_far),
+        (p_own, p_right1, p_right2, p_right3, p_far),
+    )
+
+    def remote(src, dst, chunk, send_sem, recv_sem, to):
+        part = pl.ds(chunk * size, size)
+        return pltpu.make_async_remote_copy(
+            src_ref=src.at[part],
+            dst_ref=dst.at[part],
+            send_sem=send_sem,
+            recv_sem=recv_sem,
+            device_id=(to, grp),
+            device_id_type=MESH,
+        )
+
+    def relay_in(way, step, chunk):
+        return remote(
+            ring[way][step],
+            other_ring[way][step + 1],
+            chunk,
+            ring_send.at[way, step, chunk],
+            relay_recv.at[way, step, chunk],
+            1,
+        )
+
+    def relay_out(way, step, chunk):
+        return remote(
+            other_ring[way][step],
+            ring[way][step + 1],
+            chunk,
+            relay_send.at[way, step, chunk],
+            ring_recv.at[way, step, chunk],
+            (2, n_row - 2)[way],
+        )
+
+    def direct(way, chunk):
+        return remote(
+            own,
+            ring[way][3],
+            chunk,
+            ring_send.at[way, 2, chunk],
+            ring_recv.at[way, 2, chunk],
+            (6, n_row - 6)[way],
+        )
+
+    def back_copy(which, chunk):
+        return remote(
+            held[1][which],
+            held[0][which],
+            chunk,
+            back_send.at[which, chunk],
+            back_recv.at[which, chunk],
+            partner,
+        )
+
     def halo_copy(way, slot):
         return pltpu.make_async_remote_copy(
             src_ref=window.at[slots + slot],
@@ -178,18 +252,35 @@
 
     loads["own"].wait()
 
-    @pl.when(jnp.logical_not(beside))
+    def hops(way):
+        return x if way == 0 else n_x - x
+
+    def inward(way):
+        return hops(way) == n_x - 1
+
+    def special_send(way, step, chunk):
+        pl.when(inward(way))(lambda: relay_in(way, step, chunk).start())
+        pl.when(jnp.logical_not(inward(way)))(lambda: ring_copy(way, step, chunk).start())
+
+    @pl.when(jnp.logical_not(special))
     def _():
         for i in range(CHUNKS):
             for way in range(2):
                 ring_copy(way, 0, ORDER[way][i]).start()
 
-    for way, away in enumerate((1, n_x - 1)):
-
-        @pl.when(jnp.logical_and(beside, x == away))
-        def _():
-            for chunk in ORDER[way]:
-                ring_copy(way, 0, chunk).start()
+    @pl.when(special)
+    def _():
+        for i in range(CHUNKS):
+            for way in range(2):
+                special_send(way, 0, ORDER[way][i])
+
+    @pl.when(first)
+    def _():
+        for chunk in range(CHUNKS):
+            core_copy(0, chunk).start()
+        for i in range(CHUNKS):
+            for way in range(2):
+                direct(way, ORDER[way][i]).start()
 
     def dot(a, b, dims):
         return lax.dot_general(a, b, (dims, ((), ())), preferred_element_type=F32)
@@ -237,26 +328,34 @@
     other = (p_own, p_left1, p_right1, p_left2, p_right2, left3, right3)
     last = (far, p_far, p_left3, p_right3)
 
-    def forward(way, step, chunk):
-        if step < 2 or (step == 2 and chunk in ORDER[way][: CHUNKS // 2]):
-            ring_copy(way, step + 1, chunk).start()
+    def goes_on(way, step, chunk):
+        return step < 2 or (step == 2 and chunk in ORDER[way][: CHUNKS // 2])
 
     def arrive(way, step, chunk):
         ring_copy(way, step, chunk).wait_recv()
-        forward(way, step, chunk)
+        if goes_on(way, step, chunk):
+            ring_copy(way, step + 1, chunk).start()
+
+    def pass_on(way, step, chunk):
+        relay_in(way, step, chunk).wait_recv()
+        if goes_on(way, step, chunk):
+            relay_out(way, step + 1, chunk).start()
 
     def share(way, step, chunk):
         core_copy(place[way][step], chunk).start()
+
+    def give_back(way, step, chunk):
+        back_copy(place[way][step], chunk).start()
 
     def share_all(which):
         for w in which:
             for chunk in whole:
                 core_copy(w, chunk).start()
 
-    def settle(which):
+    def settle(which, copy=core_copy):
         for w in which:
             for chunk in whole:
-                core_copy(w, chunk).wait_recv()
+                copy(w, chunk).wait_recv()
 
     def each(step, part, *acts):
         for i in part:
@@ -264,83 +363,115 @@
                 for act in acts:
                     act(way, step, ORDER[way][i])
 
-    @pl.when(jnp.logical_not(special))
-    def _():
-        each(0, whole, arrive)
-        each(1, whole, arrive)
-        fock(near)
-        each(2, half, arrive)
-        pl.when(core == 1)(lambda: pl.semaphore_wait(ready.at[2], 1))
-        share_all(range(5))
-        each(2, half, share)
-
+    def send_late():
         @pl.when(down_late)
         def _():
             pl.semaphore_wait(ready.at[1], 1)
             send_halo(1, range(slots))
 
+    def sent(copy, steps):
+        for step in steps:
+            for way in range(2):
+                for chunk in chunks(way, step):
+                    copy(way, step, chunk).wait_send()
+
+    def shared(copy, which):
+        for w in which:
+            for chunk in whole:
+                copy(w, chunk).wait_send()
+
+    @pl.when(usual)
+    def _():
+        each(0, whole, arrive)
+        each(1, whole, arrive)
+        fock(near)
+        each(2, half[:1], arrive)
+        send_late()
+        each(2, half[1:], arrive)
+        pl.when(core == 1)(lambda: pl.semaphore_wait(ready.at[2], 1))
+        share_all(range(5))
+        each(2, half, share)
         each(2, rest, arrive, share)
         each(3, half, arrive, share)
         settle(range(5))
         fock(other)
         settle(range(5, 8))
         fock(last)
-
-    def hops(way):
-        return x if way == 0 else n_x - x
+        sent(ring_copy, range(4))
+        shared(core_copy, range(8))
 
     @pl.when(special)
     def _():
+        for chunk in whole:
+            core_copy(0, chunk).start()
         for step in range(4):
             for i in range(len(chunks(0, step))):
                 for way in range(2):
-
-                    @pl.when(hops(way) > step + 1)
+                    chunk = ORDER[way][i]
+
+                    @pl.when(hops(way) != step + 1)
                     def _():
-                        ring_copy(way, step, ORDER[way][i]).wait_recv()
-                        pl.when(hops(way) < n_x - 1)(
-                            functools.partial(forward, way, step, ORDER[way][i])
-                        )
-
-        share_all((0,))
+                        ring_copy(way, step, chunk).wait_recv()
+                        if goes_on(way, step, chunk):
+                            special_send(way, step + 1, chunk)
+                        share(way, step, chunk)
+
         for step in range(4):
             for way in range(2):
 
-                @pl.when(hops(way) > step + 1)
+                @pl.when(hops(way) == step + 1)
                 def _():
                     for chunk in chunks(way, step):
-                        share(way, step, chunk)
-
-        pl.when(beside)(lambda: pl.semaphore_wait(ready.at[3], 1))
-        for way in range(2):
-
-            @pl.when(hops(way) == n_x - 1)
-            def _():
-                for step in range(4):
-                    for chunk in chunks(way, step):
-                        ring_copy(way, step, chunk).start()
-
-        for step in range(4):
-            for way in range(2):
-
-                @pl.when(hops(way) <= step + 1)
-                def _():
-                    for chunk in chunks(way, step):
-                        arrive(way, step, chunk)
+                        if step == 1:
+                            ring_copy(way, step, chunk).wait_recv()
+                        else:
+                            arrive(way, step, chunk)
                         share(way, step, chunk)
 
         settle(range(8))
         fock(near)
         fock(other)
         fock(last)
-
-    for way in range(2):
+        sent(ring_copy, (0, 1, 3))
+        for way in range(2):
+
+            @pl.when(hops(way) != 2)
+            def _():
+                for chunk in whole:
+                    ring_copy(way, 2, chunk).wait_send()
+
+        shared(core_copy, range(8))
+
+    @pl.when(relay)
+    def _():
+        for step in range(3):
+            each(step, whole, arrive, pass_on)
+        each(3, half, arrive, pass_on)
+        pl.semaphore_wait(ready.at[2], 1)
+        share_all((0,))
         for step in range(4):
-            for chunk in chunks(way, step):
-                ring_copy(way, step, chunk).wait_send()
-    for which in range(8):
-        for chunk in whole:
-            core_copy(which, chunk).wait_send()
+            each(step, whole if step < 3 else half, share, give_back)
+        settle((0,))
+        fock(near)
+        fock(other)
+        fock(last)
+        sent(ring_copy, range(4))
+        sent(relay_out, range(1, 4))
+        shared(core_copy, range(8))
+        shared(back_copy, range(1, 8))
+
+    @pl.when(first)
+    def _():
+        settle(range(8))
+        settle(range(1, 8), back_copy)
+        fock(near)
+        fock(other)
+        fock(last)
+        sent(ring_copy, (0,))
+        for way in range(2):
+            for chunk in whole:
+                direct(way, chunk).wait_send()
+        shared(core_copy, (0,))
 
     def take_halo(way):
         for s in range(slots):
@@ -394,9 +525,13 @@
                 pltpu.SemaphoreType.DMA((2, 4, CHUNKS)),
                 pltpu.SemaphoreType.DMA((8, CHUNKS)),
                 pltpu.SemaphoreType.DMA((8, CHUNKS)),
+                pltpu.SemaphoreType.DMA((2, 4, CHUNKS)),
+                pltpu.SemaphoreType.DMA((2, 4, CHUNKS)),
+                pltpu.SemaphoreType.DMA((8, CHUNKS)),
+                pltpu.SemaphoreType.DMA((8, CHUNKS)),
                 pltpu.SemaphoreType.DMA((2, slots)),
                 pltpu.SemaphoreType.DMA((2, slots)),
-                pltpu.SemaphoreType.REGULAR((4,)),
+                pltpu.SemaphoreType.REGULAR((3,)),
             ],
             compiler_params=pltpu.CompilerParams(
                 collective_id=0, has_side_effects=True, vmem_limit_bytes=16 << 20

time: 44.7 us -> 41.4 us (0.926)
  the two profiles are of different devices: /device:TPU:1 before, /device:TPU:13 now
where the time goes in v5:
time: 41.4 us; the launch traced here: 41.2 us
  Pallas kernels  39.6 us (96%)
  local copies, waits for them, and re-layouts  0.97 us (2%)
  between operations  0.66 us (2%)
    pallas_call x1, Pallas kernels, local(): pl.pallas_call(functools.partial(kernel, n_row, n_grp), out_shape=jax.Sha...  39.6 us
    unnamed x1, local copies, waits for them, and re-layouts  0.97 us

profile of v5, /device:TPU:13, one launch (start us, length us, event | category | flops | bytes accessed | tf_op | source)
XLA Modules:
  0.0 41.2 jit_solution(107038802428932903)
XLA Ops:
  0.7 39.6 %shard_map.91 = f32[4,256,256]{2,1,0:T(8,128)S(1)} custom-call(bf16[16,32,256]{2,1,0:T(8,128)(2,1)} %ints_hbm.1, bf16[4,256,256]{2,1,0:T(8,128)(2,1)} %amps_hbm.1, bf16[4,256,256]{2,1,0:T(8,128)(2,1)} %bases_hbm.1, s32[2,4]{1,0:T(2,128)} %bitcast.2, s32[1,1]{1,0:T(1,128)S(6)} %copy.11.count_ref, s32[4,4]{1,0:T(4,128)} %neigh_hbm.1, f32[4,4]{1,0:T(4,128)} %coup_hbm.1, ...), custom_call_target="tpu_custom_call" | custom-call | tf_op jit(solution)/shard_map/pallas_call | solution.py:506
  40.3 1.0 %copy.12 = f32[4,256,256]{2,1,0:T(8,128)} copy(f32[4,256,256]{2,1,0:T(8,128)S(1)} %shard_map.91) | data formatting | bytes 2097152

commit v6 on v2

--- a/solution.py
+++ b/solution.py
@@ -117,8 +117,6 @@
     pl.when(down_early)(lambda: signal(ready.at[0], row, halo_to[1]))
 
     ring = ((own, left1, left2, left3), (own, right1, right2, right3))
-    sends = []
-
     def ring_copy(way, step, chunk):
         src = ring[way][step]
         dst = ring[way][step + 1] if step < 3 else far
@@ -126,8 +124,8 @@
         return pltpu.make_async_remote_copy(
             src_ref=src.at[part],
             dst_ref=dst.at[part],
-            send_sem=ring_send.at[way, step, chunk],
-            recv_sem=ring_recv.at[way, step, chunk],
+            send_sem=ring_send.at[way],
+            recv_sem=ring_recv.at[way, step * CHUNKS + ORDER[way].index(chunk)],
             device_id=(ring_to[way], grp),
             device_id_type=MESH,
         )
@@ -144,31 +142,40 @@
     )
     place = ((1, 3, 5, 7), (2, 4, 6, 7))
 
-    def core_copy(which, chunk):
+    def core_copy(which, chunk=None):
         src, dst = pairs[which]
-        part = pl.ds(chunk * size, size)
+        part = pl.ds(0, orbs) if chunk is None else pl.ds(chunk * size, size)
         return pltpu.make_async_remote_copy(
             src_ref=src.at[part],
             dst_ref=dst.at[part],
-            send_sem=core_send.at[which, chunk],
-            recv_sem=core_recv.at[which, chunk],
+            send_sem=core_send.at[which // 4],
+            recv_sem=core_recv.at[which // 5],
             device_id=(partner, grp),
             device_id_type=MESH,
         )
 
-    def halo_copy(way, slot):
+    def tile_bytes(tiles, send_sem, recv_sem):
         return pltpu.make_async_remote_copy(
-            src_ref=window.at[slots + slot],
-            dst_ref=window.at[(0 if way == 0 else 2 * slots) + slot],
-            send_sem=halo_send.at[way, slot],
-            recv_sem=halo_recv.at[way, slot],
+            src_ref=window.at[pl.ds(0, tiles)],
+            dst_ref=window.at[pl.ds(0, tiles)],
+            send_sem=send_sem,
+            recv_sem=recv_sem,
+            device_id=(partner, grp),
+            device_id_type=MESH,
+        )
+
+    def halo_copy(way, slot=0, tiles=1):
+        return pltpu.make_async_remote_copy(
+            src_ref=window.at[pl.ds(slots + slot, tiles)],
+            dst_ref=window.at[pl.ds((0 if way == 0 else 2 * slots) + slot, tiles)],
+            send_sem=halo_send.at[way],
+            recv_sem=halo_recv.at[way],
             device_id=(row, halo_to[way]),
             device_id_type=MESH,
         )
 
     def start(copy):
         copy.start()
-        sends.append(copy)
 
     loads[2].wait()
     for i in range(CHUNKS):
@@ -233,9 +240,8 @@
     def share(way, step, chunk):
         start(core_copy(place[way][step], chunk))
 
-    def settle(which):
-        for chunk in range(CHUNKS):
-            core_copy(which, chunk).wait_recv()
+    def settle(group):
+        tile_bytes(2 * (5, 3)[group], core_send.at[0], core_recv.at[group]).wait_recv()
 
     for step in range(2):
         for i in range(CHUNKS):
@@ -263,20 +269,15 @@
         for way in range(2):
             arrive(way, 2, ORDER[way][i], False)
             share(way, 2, ORDER[way][i])
-    for which in range(5):
-        settle(which)
-    fock((p_own, p_left1, p_right1, p_left2, p_right2, left3, right3))
     for i in range(CHUNKS // 2):
         for way in range(2):
             arrive(way, 3, ORDER[way][i], False)
             share(way, 3, ORDER[way][i])
-    for which in range(5, 8):
-        settle(which)
-    fock((far, p_far, p_left3, p_right3))
+    settle(0)
+    fock((p_own, p_left1, p_right1, p_left2, p_right2, left3, right3))
 
     def take_halo(way):
-        for s in range(slots):
-            halo_copy(way, s).wait_recv()
+        halo_copy(way, 0, slots).wait_recv()
 
     pl.when(has_up)(functools.partial(take_halo, 1))
     pl.when(has_down)(functools.partial(take_halo, 0))
@@ -287,14 +288,22 @@
             total = term if total is None else total + term
         back_first = dot(turned[s], total.astype(BF16), ((1,), (0,))).astype(BF16)
         back = dot(back_first, base[s], ((1,), (0,)))
-        out_ref[s] = (out_ref[s] - back) * alive[s]
-
-    for copy in sends:
-        copy.wait_send()
+        out_ref[s] -= back
+
+    settle(1)
+    lhs = jnp.concatenate([b[row] for b in (far, p_far, p_left3, p_right3)], axis=0).T
+    for s in range(slots):
+        at = orbs_ref[1, s]
+        rhs = jnp.concatenate([b[at] for b in (far, p_far, p_left3, p_right3)], axis=0)
+        out_ref[s] = (out_ref[s] + dot(lhs, rhs, ((1,), (0,)))) * alive[s]
+
+    for way in range(2):
+        tile_bytes(7, ring_send.at[way], ring_recv.at[way, 0]).wait_send()
+    for group in range(2):
+        tile_bytes(8, core_send.at[group], core_recv.at[0]).wait_send()
 
     def sent_halo(way):
-        for s in range(slots):
-            halo_copy(way, s).wait_send()
+        halo_copy(way, 0, slots).wait_send()
 
     pl.when(has_up)(functools.partial(sent_halo, 0))
     pl.when(has_down)(functools.partial(sent_halo, 1))
@@ -325,12 +334,12 @@
             + [
                 pltpu.VMEM(virt.shape, F32),
                 pltpu.SemaphoreType.DMA((len(args) - 1,)),
-                pltpu.SemaphoreType.DMA((2, 4, CHUNKS)),
-                pltpu.SemaphoreType.DMA((2, 4, CHUNKS)),
-                pltpu.SemaphoreType.DMA((8, CHUNKS)),
-                pltpu.SemaphoreType.DMA((8, CHUNKS)),
-                pltpu.SemaphoreType.DMA((2, slots)),
-                pltpu.SemaphoreType.DMA((2, slots)),
+                pltpu.SemaphoreType.DMA((2,)),
+                pltpu.SemaphoreType.DMA((2, 3 * CHUNKS + CHUNKS // 2)),
+                pltpu.SemaphoreType.DMA((2,)),
+                pltpu.SemaphoreType.DMA((2,)),
+                pltpu.SemaphoreType.DMA((2,)),
+                pltpu.SemaphoreType.DMA((2,)),
                 pltpu.SemaphoreType.REGULAR((3,)),
             ],
             compiler_params=pltpu.CompilerParams(

time: 37.4 us -> 35.6 us (0.952)
  Pallas kernels: 35.6 us -> 33.8 us
    pallas_call x1, Pallas kernels: 35.6 us -> 33.8 us  [local(): pl.pallas_call(functools.partial(kernel, n_row, n_grp), out_shape=jax.Sha...]
where the time goes in v6:
time: 35.6 us; the launch traced here: 35.5 us
  Pallas kernels  33.8 us (95%)
  local copies, waits for them, and re-layouts  0.97 us (3%)
  between operations  0.66 us (2%)
    pallas_call x1, Pallas kernels, local(): pl.pallas_call(functools.partial(kernel, n_row, n_grp), out_shape=jax.Sha...  33.8 us
    unnamed x1, local copies, waits for them, and re-layouts  0.97 us

profile of v6, /device:TPU:1, one launch (start us, length us, event | category | flops | bytes accessed | tf_op | source)
XLA Modules:
  0.0 35.5 jit_solution(6998599859984991489)
XLA Ops:
  0.7 33.8 %shard_map.91 = f32[4,256,256]{2,1,0:T(8,128)S(1)} custom-call(bf16[16,32,256]{2,1,0:T(8,128)(2,1)} %ints_hbm.1, bf16[4,256,256]{2,1,0:T(8,128)(2,1)} %amps_hbm.1, bf16[4,256,256]{2,1,0:T(8,128)(2,1)} %bases_hbm.1, s32[2,4]{1,0:T(2,128)} %bitcast.2, s32[1,1]{1,0:T(1,128)S(6)} %copy.11.count_ref, s32[4,4]{1,0:T(4,128)} %neigh_hbm.1, f32[4,4]{1,0:T(4,128)} %coup_hbm.1, ...), custom_call_target="tpu_custom_call" | custom-call | tf_op jit(solution)/shard_map/pallas_call | solution.py:319
  34.5 1.0 %copy.12 = f32[4,256,256]{2,1,0:T(8,128)} copy(f32[4,256,256]{2,1,0:T(8,128)S(1)} %shard_map.91) | data formatting | bytes 2097152

commit v7 on v6

--- a/solution.py
+++ b/solution.py
@@ -108,6 +108,27 @@
     pl.when(core == 1)(lambda: signal(barrier, partner, grp))
     pl.when(up_late)(lambda: signal(barrier, row, halo_to[0]))
     pl.when(down_late)(lambda: signal(barrier, row, halo_to[1]))
+    def dot(a, b, dims):
+        return lax.dot_general(a, b, (dims, ((), ())), preferred_element_type=F32)
+
+    alive = [jnp.where(s < count_ref[0, 0], 1.0, 0.0).astype(F32) for s in range(slots)]
+
+    def move(tiles):
+        for s in tiles:
+            u = base[s]
+            masked = (amp[s].astype(F32) * alive[s]).astype(BF16)
+            first = dot(u, masked, ((1,), (0,))).astype(BF16)
+            window[slots + s] = dot(first, u, ((1,), (1,))).astype(BF16)
+
+    def load_tiles():
+        loads[0].wait()
+        loads[1].wait()
+
+    @pl.when(z == N_Z - 1)
+    def _():
+        load_tiles()
+        move((0, 1))
+
     pl.semaphore_wait(
         barrier,
         2 + (1 - core) + jnp.where(up_early, 1, 0) + jnp.where(down_early, 1, 0),
@@ -177,39 +198,30 @@
     def start(copy):
         copy.start()
 
-    loads[2].wait()
-    for i in range(CHUNKS):
-        for way in range(2):
-            start(ring_copy(way, 0, ORDER[way][i]))
-    def dot(a, b, dims):
-        return lax.dot_general(a, b, (dims, ((), ())), preferred_element_type=F32)
-
-    for load in loads[:2] + loads[3:]:
-        load.wait()
-    count = count_ref[0, 0]
-    alive = [jnp.where(s < count, 1.0, 0.0).astype(F32) for s in range(slots)]
-
     def send_halo(way, tiles):
         for s in tiles:
             halo_copy(way, s).start()
 
-    for s in range(slots):
-        u = base[s]
-        masked = (amp[s].astype(F32) * alive[s]).astype(BF16)
-        first = dot(u, masked, ((1,), (0,))).astype(BF16)
-        window[slots + s] = dot(first, u, ((1,), (1,))).astype(BF16)
-        if s > 0:
-            pl.when(up_early)(functools.partial(send_halo, 0, (s - 1,)))
-            pl.when(down_early)(functools.partial(send_halo, 1, (s - 1,)))
+    def send_early(tiles):
+        pl.when(up_early)(functools.partial(send_halo, 0, tiles))
+        pl.when(down_early)(functools.partial(send_halo, 1, tiles))
+
+    pl.when(z == N_Z - 1)(lambda: send_early((0, 1)))
+    loads[2].wait()
+    for i in range(CHUNKS):
+        for way in range(2):
+            start(ring_copy(way, 0, ORDER[way][i]))
+    @pl.when(z != N_Z - 1)
+    def _():
+        load_tiles()
+        move((0, 1))
+        send_early((0, 1))
+
+    move((2, 3))
+    send_early((2, 3))
+    for load in loads[3:]:
+        load.wait()
     turned[0] = base[0].T
-    pl.when(up_early)(functools.partial(send_halo, 0, (slots - 1,)))
-    pl.when(down_early)(functools.partial(send_halo, 1, (slots - 1,)))
-
-    @pl.when(up_late)
-    def _():
-        pl.semaphore_wait(ready.at[0], 1)
-        send_halo(0, range(slots))
-
     for s in range(1, slots):
         turned[s] = base[s].T
     energy = jnp.transpose(virt_ref[...])
@@ -243,11 +255,18 @@
     def settle(group):
         tile_bytes(2 * (5, 3)[group], core_send.at[0], core_recv.at[group]).wait_recv()
 
-    for step in range(2):
-        for i in range(CHUNKS):
-            for way in range(2):
-                arrive(way, step, ORDER[way][i], True)
-    fock((own, left1, right1, left2, right2))
+    for i in range(CHUNKS):
+        for way in range(2):
+            arrive(way, 0, ORDER[way][i], True)
+
+    @pl.when(up_late)
+    def _():
+        pl.semaphore_wait(ready.at[0], 1)
+        send_halo(0, range(slots))
+
+    for i in range(CHUNKS):
+        for way in range(2):
+            arrive(way, 1, ORDER[way][i], True)
     for i in range(CHUNKS // 2):
         for way in range(2):
             arrive(way, 2, ORDER[way][i], True)
@@ -273,6 +292,7 @@
         for way in range(2):
             arrive(way, 3, ORDER[way][i], False)
             share(way, 3, ORDER[way][i])
+    fock((own, left1, right1, left2, right2))
     settle(0)
     fock((p_own, p_left1, p_right1, p_left2, p_right2, left3, right3))
 

time: 35.6 us -> 35.3 us (level)
  no operation moved by 1% of the time
where the time goes in v7:
time: 35.3 us; the launch traced here: 35.1 us
  Pallas kernels  33.5 us (95%)
  local copies, waits for them, and re-layouts  0.97 us (3%)
  between operations  0.66 us (2%)
    pallas_call x1, Pallas kernels, local(): pl.pallas_call(functools.partial(kernel, n_row, n_grp), out_shape=jax.Sha...  33.5 us
    unnamed x1, local copies, waits for them, and re-layouts  0.97 us

profile of v7, /device:TPU:1, one launch (start us, length us, event | category | flops | bytes accessed | tf_op | source)
XLA Modules:
  0.0 35.1 jit_solution(16113574711000933267)
XLA Ops:
  0.7 33.5 %shard_map.91 = f32[4,256,256]{2,1,0:T(8,128)S(1)} custom-call(bf16[16,32,256]{2,1,0:T(8,128)(2,1)} %ints_hbm.1, bf16[4,256,256]{2,1,0:T(8,128)(2,1)} %amps_hbm.1, bf16[4,256,256]{2,1,0:T(8,128)(2,1)} %bases_hbm.1, s32[2,4]{1,0:T(2,128)} %bitcast.2, s32[1,1]{1,0:T(1,128)S(6)} %copy.11.count_ref, s32[4,4]{1,0:T(4,128)} %neigh_hbm.1, f32[4,4]{1,0:T(4,128)} %coup_hbm.1, ...), custom_call_target="tpu_custom_call" | custom-call | tf_op jit(solution)/shard_map/pallas_call | solution.py:339
  34.2 1.0 %copy.12 = f32[4,256,256]{2,1,0:T(8,128)} copy(f32[4,256,256]{2,1,0:T(8,128)S(1)} %shard_map.91) | data formatting | bytes 2097152

commit v8 on v7

--- a/solution.py
+++ b/solution.py
@@ -71,24 +71,6 @@
     partner = row + 1 - 2 * (row % 2)
     halo_to = ((grp + 1) % n_grp, (grp + n_grp - 1) % n_grp)
 
-    loads = [
-        pltpu.make_async_copy(src, dst, local_sem.at[i])
-        for i, (src, dst) in enumerate(
-            (
-                (bases_hbm, base),
-                (amps_hbm, amp),
-                (ints_hbm, own),
-                (orbs_hbm, orbs_ref),
-                (neigh_hbm, neigh_ref),
-                (coup_hbm, coup_ref),
-                (occ_hbm, occ_ref),
-                (virt_hbm, virt_ref),
-            )
-        )
-    ]
-    for load in loads:
-        load.start()
-
     core, z = row % 2, grp % N_Z
     has_up, has_down = grp < n_grp - 1, grp > 0
     up_first = jnp.logical_or(z == N_Z - 1, jnp.logical_and(row == 0, grp == 0))
@@ -108,6 +90,24 @@
     pl.when(core == 1)(lambda: signal(barrier, partner, grp))
     pl.when(up_late)(lambda: signal(barrier, row, halo_to[0]))
     pl.when(down_late)(lambda: signal(barrier, row, halo_to[1]))
+    loads = [
+        pltpu.make_async_copy(src, dst, local_sem.at[i])
+        for i, (src, dst) in enumerate(
+            (
+                (ints_hbm, own),
+                (bases_hbm, base),
+                (amps_hbm, amp),
+                (orbs_hbm, orbs_ref),
+                (neigh_hbm, neigh_ref),
+                (coup_hbm, coup_ref),
+                (occ_hbm, occ_ref),
+                (virt_hbm, virt_ref),
+            )
+        )
+    ]
+    for load in loads:
+        load.start()
+
     def dot(a, b, dims):
         return lax.dot_general(a, b, (dims, ((), ())), preferred_element_type=F32)
 
@@ -121,8 +121,8 @@
             window[slots + s] = dot(first, u, ((1,), (1,))).astype(BF16)
 
     def load_tiles():
-        loads[0].wait()
         loads[1].wait()
+        loads[2].wait()
 
     @pl.when(z == N_Z - 1)
     def _():
@@ -207,7 +207,7 @@
         pl.when(down_early)(functools.partial(send_halo, 1, tiles))
 
     pl.when(z == N_Z - 1)(lambda: send_early((0, 1)))
-    loads[2].wait()
+    loads[0].wait()
     for i in range(CHUNKS):
         for way in range(2):
             start(ring_copy(way, 0, ORDER[way][i]))

time: 35.3 us -> 35.2 us (level)
  no operation moved by 1% of the time
where the time goes in v8:
time: 35.2 us; the launch traced here: 35.1 us
  Pallas kernels  33.4 us (95%)
  local copies, waits for them, and re-layouts  0.97 us (3%)
  between operations  0.66 us (2%)
    pallas_call x1, Pallas kernels, local(): pl.pallas_call(functools.partial(kernel, n_row, n_grp), out_shape=jax.Sha...  33.4 us
    unnamed x1, local copies, waits for them, and re-layouts  0.97 us

profile of v8, /device:TPU:1, one launch (start us, length us, event | category | flops | bytes accessed | tf_op | source)
XLA Modules:
  0.0 35.1 jit_solution(17302912308909069386)
XLA Ops:
  0.7 33.4 %shard_map.91 = f32[4,256,256]{2,1,0:T(8,128)S(1)} custom-call(bf16[16,32,256]{2,1,0:T(8,128)(2,1)} %ints_hbm.1, bf16[4,256,256]{2,1,0:T(8,128)(2,1)} %amps_hbm.1, bf16[4,256,256]{2,1,0:T(8,128)(2,1)} %bases_hbm.1, s32[2,4]{1,0:T(2,128)} %bitcast.2, s32[1,1]{1,0:T(1,128)S(6)} %copy.11.count_ref, s32[4,4]{1,0:T(4,128)} %neigh_hbm.1, f32[4,4]{1,0:T(4,128)} %coup_hbm.1, ...), custom_call_target="tpu_custom_call" | custom-call | tf_op jit(solution)/shard_map/pallas_call | solution.py:339
  34.1 1.0 %copy.12 = f32[4,256,256]{2,1,0:T(8,128)} copy(f32[4,256,256]{2,1,0:T(8,128)S(1)} %shard_map.91) | data formatting | bytes 2097152
